TPU v7x, 32 devices: a whole 2x2x4 slice. The times are simulated.
32 devices in a mesh: gx: 4 (over x, core), gy: 8 (over z, y).
Axes of the slice: x: 2, y: 2, z: 4, core: 2. Of those that a mesh axis runs over, the one named last changes fastest.
Arguments:
- tokens: bfloat16 [256, 8192], P('gy', 'gx'), may hold values from -6 to 6
- up_old: bfloat16 [8192, 8192], P(('gx', 'gy')), may hold values from -0.0625 to 0.0625
- down_old: bfloat16 [8192, 8192], P(('gx', 'gy')), may hold values from -0.125 to 0.125
- old_slot: int32 [64], replicated, may hold values from 0 to 63, as said below
- new_owner: int32 [64], replicated, may hold values from 0 to 31, as said below
- hot_rank: int32 [64], replicated, may hold values from 0 to 1, as said below
- route: int32 [256], replicated, may hold values from 0 to 255, each once
Outputs:
- up_new: bfloat16 [8192, 8192], P(('gx', 'gy'))
- down_new: bfloat16 [8192, 8192], P(('gx', 'gy'))
- mixed: bfloat16 [256, 8192], P('gy', 'gx')
Inputs may be any that keep to these rules, and one draw needn't show every extreme that they name: `old_slot`: each slot number appears exactly once. `new_owner`: each device index is the new owner of exactly 2 blocks. `hot_rank`: the blocks of one new owner have distinct ranks.
All inputs are finite; a program needn't handle non-finite values.
Results may differ from a plain program's by a relative error of at most 0.0049.
Values may be sent and summed in bfloat16 or wider, within the bound.
No kernel may reach another device: no remote copies, remote signals or barrier semaphores. Data moves between devices by JAX's collectives and lax.ppermute only.
A program may use at most 128 MiB of HBM per device.

v0:
```python
import jax
import jax.numpy as jnp
from jax import lax
from jax.sharding import PartitionSpec as P

BLOCK = 128


def layer_terms(ordered, up_rows, down_rows):
    pre = lax.dot_general(
        ordered, up_rows, (((1,), (1,)), ((), ())), preferred_element_type=jnp.float32
    )
    hidden = jax.nn.gelu(pre, approximate=False).astype(jnp.bfloat16)
    return jnp.dot(hidden, down_rows, preferred_element_type=jnp.float32)


def relocate(up_old, down_old, old_slot, new_owner, hot_rank):
    held = up_old.shape[0] // BLOCK
    width = up_old.shape[1]
    shaped = (up_old.reshape(held, BLOCK, width), down_old.reshape(held, BLOCK, width))
    spread = (
        lax.all_to_all(shaped[0], ("gx", "gy"), split_axis=1, concat_axis=0, tiled=True),
        lax.all_to_all(shaped[1], ("gx", "gy"), split_axis=1, concat_axis=0, tiled=True),
    )
    total = spread[0].shape[0]
    new_slot = new_owner * held + hot_rank
    source = jnp.zeros((total,), jnp.int32).at[new_slot].set(old_slot)
    picked = (jnp.take(spread[0], source, axis=0), jnp.take(spread[1], source, axis=0))
    landed = (
        lax.all_to_all(picked[0], ("gx", "gy"), split_axis=0, concat_axis=1, tiled=True),
        lax.all_to_all(picked[1], ("gx", "gy"), split_axis=0, concat_axis=1, tiled=True),
    )
    return (landed[0].reshape(held * BLOCK, width), landed[1].reshape(held * BLOCK, width))


def shards(tokens, up_old, down_old, old_slot, new_owner, hot_rank, route):
    feature_rows = lax.all_gather(tokens, "gx", axis=1, tiled=True)
    everyone = lax.all_gather(feature_rows, "gy", axis=0, tiled=True)
    ordered = jnp.take(everyone, route, axis=0)
    partial_out = layer_terms(ordered, up_old, down_old)
    up_new, down_new = relocate(up_old, down_old, old_slot, new_owner, hot_rank)
    by_columns = lax.psum_scatter(partial_out, "gx", scatter_dimension=1, tiled=True)
    summed = lax.psum_scatter(by_columns, "gy", scatter_dimension=0, tiled=True)
    return (up_new, down_new, summed.astype(jnp.bfloat16))


def solution(mesh):
    in_specs = (P("gy", "gx"), P(("gx", "gy"), None), P(("gx", "gy"), None), P(), P(), P(), P())
    out_specs = (P(("gx", "gy"), None), P(("gx", "gy"), None), P("gy", "gx"))
    return jax.shard_map(shards, mesh=mesh, in_specs=in_specs, out_specs=out_specs, check_vma=False)
```

profile of v0, /device:TPU:0, one launch (start us, length us, event | category | flops | bytes accessed | tf_op | source)
XLA Modules:
  0.0 539.3 jit_solution(7738522427065044836)
XLA Ops:
  7.2 8.6 %copy.13 = bf16[2,128,8192]{2,0,1:T(2,128)(2,1)} copy(bf16[2,128,8192]{2,1,0:T(8,128)(2,1)} %bitcast.20) | data formatting | bytes 8388608 | tf_op jit(solution)/shard_map/reshape | solution.py:20
  15.7 7.5 %all-to-all-start.2 = ((bf16[2,128,8192]{2,0,1:T(2,128)(2,1)}), bf16[2,128,8192]{2,0,1:T(2,128)(2,1)}, u32[]{:S(2)}, u32[]{:S(2)}) async-start(bf16[2,128,8192]{2,0,1:T(2,128)(2,1)} %copy.13), calls=%async_computation.2 | async-start | bytes 8388608 | tf_op jit(solution)/shard_map/all_to_all | solution.py:23
  23.3 29.0 %all_gather.6 = bf16[32,8192]{1,0:T(8,128)(2,1)} all-gather(bf16[32,2048]{1,0:T(8,128)(2,1)S(1)} %copy-done), channel_id=1, replica_groups=mesh['gx'=4,'gy'=8] {'gx'}, dimensions={1}, use_global_device_ids=true | all-gather | bytes 655360 | tf_op jit(solution)/shard_map/all_gather | solution.py:37
  52.3 8.6 %copy.10 = bf16[2,128,8192]{2,0,1:T(2,128)(2,1)} copy(bf16[2,128,8192]{2,1,0:T(8,128)(2,1)} %bitcast.19) | data formatting | bytes 8388608 | tf_op jit(solution)/shard_map/reshape | solution.py:20
  60.8 100.0 %all-to-all-done.2 = bf16[2,128,8192]{2,0,1:T(2,128)(2,1)} async-done(((bf16[2,128,8192]{2,0,1:T(2,128)(2,1)}), bf16[2,128,8192]{2,0,1:T(2,128)(2,1)}, u32[]{:S(2)}, u32[]{:S(2)}) %all-to-all-start.2) | async-done | bytes 4194336 | tf_op jit(solution)/shard_map/all_to_all | solution.py:23
  160.9 4.8 all-to-all-start
  166.0 8.7 %all-gather.2.cloned.1.call-done = bf16[256,8192]{1,0:T(8,128)(2,1)} async-done(((bf16[32,8192]{1,0:T(8,128)(2,1)}), bf16[256,8192]{1,0:T(8,128)(2,1)}) %all-gather.2.cloned.1.call-update) | async-done | bytes 4194320 | tf_op jit(solution)/shard_map/all_gather | solution.py:38
  174.7 11.7 %gather_fusion = bf16[256,8192]{1,0:T(8,128)(2,1)} fusion(bf16[256,8192]{1,0:T(8,128)(2,1)} %all-gather.2.cloned.1.call-done, s32[1024]{0:T(1024)S(1)} %pad_clamp_fusion), kind=kCustom, calls=%fused_computation.2 | custom fusion | bytes 8389632 | tf_op jit(solution)/shard_map/jit(_take)/gather | solution.py:39
  186.4 13.0 %fusion.17 = f32[256,8192]{1,0:T(8,128)} fusion(bf16[256,8192]{1,0:T(8,128)(2,1)} %param.11, bf16[256,8192]{1,0:T(8,128)(2,1)} %param.10, bf16[256,8192]{1,0:T(8,128)(2,1)} %gather_fusion, pred[256]{0:T(512)(128)(4,1)S(1)} %compare_and_fusion.1), kind=kOutput, calls=%fused_computation.29 | convolution fusion | flops 2153840640 | bytes 20971776 | tf_op jit(solution)/shard_map/dot_general | solution.py:14
  200.1 1.1 scatter_custom_fusion
  201.2 8.8 %copy.14 = bf16[32,2,4,8192]{3,2,1,0:T(4,128)(2,1)} copy(bf16[32,2,4,8192]{3,1,2,0:T(2,128)(2,1)} %bitcast.8) | data formatting | bytes 8388608 | tf_op jit(solution)/shard_map/all_to_all | solution.py:23
  210.0 51.5 %all-to-all-done = bf16[2,128,8192]{2,0,1:T(2,128)(2,1)} async-done(((bf16[2,128,8192]{2,0,1:T(2,128)(2,1)}), bf16[2,128,8192]{2,0,1:T(2,128)(2,1)}, u32[]{:S(2)}, u32[]{:S(2)}) %all-to-all-start) | async-done | bytes 4194336 | tf_op jit(solution)/shard_map/all_to_all | solution.py:22
  261.5 8.1 %copy.11 = bf16[32,2,4,8192]{3,2,1,0:T(4,128)(2,1)} copy(bf16[32,2,4,8192]{3,1,2,0:T(2,128)(2,1)} %bitcast.2) | data formatting | bytes 8388608 | tf_op jit(solution)/shard_map/all_to_all | solution.py:22
  269.6 8.8 %gather_fusion.2 = bf16[64,4,8192]{2,1,0:T(4,128)(2,1)} fusion(bf16[64,4,8192]{2,1,0:T(4,128)(2,1)} %bitcast.22, s32[1024]{0:T(1024)S(1)} %pad_clamp_fusion.1), kind=kCustom, calls=%fused_computation.1.clone | custom fusion | bytes 8388864 | tf_op jit(solution)/shard_map/jit(_take)/gather | solution.py:28
  278.4 8.5 %gather_fusion.1 = bf16[64,4,8192]{2,1,0:T(4,128)(2,1)} fusion(bf16[64,4,8192]{2,1,0:T(4,128)(2,1)} %bitcast.23, s32[1024]{0:T(1024)S(1)} %pad_clamp_fusion.1), kind=kCustom, calls=%fused_computation.clone | custom fusion | bytes 8388864 | tf_op jit(solution)/shard_map/jit(_take)/gather | solution.py:28
  287.0 7.6 %broadcast_select_fusion = (bf16[64,4,8192]{2,1,0:T(4,128)(2,1)S(1)}, bf16[64,4,8192]{2,1,0:T(4,128)(2,1)}) fusion(bf16[64,4,8192]{2,1,0:T(4,128)(2,1)} %gather_fusion.2, pred[64]{0:T(512)(128)(4,1)S(1)} %compare_and_fusion, bf16[64,4,8192]{2,1,0:T(4,128)(2,1)} %gather_fusion.1), kind=kLoop, calls=%fused_computation.6 | loop fusion | flops 4194304 | bytes 16777280 | tf_op jit(solution)/shard_map/jit(_take)/select_n | solution.py:28
  294.6 97.3 %all_to_all.66 = bf16[64,4,8192]{2,1,0:T(4,128)(2,1)} all-to-all(bf16[64,4,8192]{2,1,0:T(4,128)(2,1)S(1)} %get-tuple-element.4), channel_id=1, replica_groups=mesh['gx'=4,'gy'=8] {'gx','gy'}, dimensions={0} | all-to-all | bytes 8388608 | tf_op jit(solution)/shard_map/all_to_all | solution.py:31
  391.9 3.6 all-to-all-start.1
  396.3 7.3 %copy.15 = bf16[2,32,4,8192]{3,2,1,0:T(4,128)(2,1)} copy(bf16[2,32,4,8192]{3,2,0,1:T(4,128)(2,1)} %bitcast.21) | data formatting | bytes 8388608 | tf_op jit(solution)/shard_map/all_to_all | solution.py:31
  403.5 6.9 %reshape.33 = bf16[256,8192]{1,0:T(8,128)(2,1)} reshape(bf16[2,32,4,8192]{3,2,1,0:T(4,128)(2,1)} %copy.15) | data formatting | bytes 8388608 | tf_op jit(solution)/shard_map/reshape | solution.py:33
  410.4 106.2 %all-to-all-done.1 = bf16[64,4,8192]{2,1,0:T(4,128)(2,1)} async-done(((bf16[64,4,8192]{2,1,0:T(4,128)(2,1)}), bf16[64,4,8192]{2,1,0:T(4,128)(2,1)}, u32[]{:S(2)}, u32[]{:S(2)}) %all-to-all-start.1) | async-done | bytes 4194336 | tf_op jit(solution)/shard_map/all_to_all | solution.py:30
  516.6 7.2 %copy.12 = bf16[2,32,4,8192]{3,2,1,0:T(4,128)(2,1)} copy(bf16[2,32,4,8192]{3,2,0,1:T(4,128)(2,1)} %bitcast.5) | data formatting | bytes 8388608 | tf_op jit(solution)/shard_map/all_to_all | solution.py:30
  523.8 6.9 %reshape.31 = bf16[256,8192]{1,0:T(8,128)(2,1)} reshape(bf16[2,32,4,8192]{3,2,1,0:T(4,128)(2,1)} %copy.12) | data formatting | bytes 8388608 | tf_op jit(solution)/shard_map/reshape | solution.py:33
  530.7 1.6 convert_element_type.7
  (23 shorter events, 1.7 us)
Async XLA Ops:
  15.7 7.5 %copy-start = (bf16[32,2048]{1,0:T(8,128)(2,1)S(1)}, bf16[32,2048]{1,0:T(8,128)(2,1)}, u32[]{:S(2)}) copy-start(bf16[32,2048]{1,0:T(8,128)(2,1)} %param.9) | copy-start | bytes 393220
  15.7 145.1 %all-to-all-start.2 = ((bf16[2,128,8192]{2,0,1:T(2,128)(2,1)}), bf16[2,128,8192]{2,0,1:T(2,128)(2,1)}, u32[]{:S(2)}, u32[]{:S(2)}) async-start(bf16[2,128,8192]{2,0,1:T(2,128)(2,1)} %copy.13), calls=%async_computation.2 | async-start | bytes 8388608 | tf_op jit(solution)/shard_map/all_to_all | solution.py:23
  23.2 151.5 %all-gather.2.cloned.1.call-start = ((), (), s32[]{:S(2)}) async-start(), calls=%async_computation.6 | async-start | bytes 4718592 | tf_op jit(solution)/shard_map/all_gather | solution.py:38
  60.8 105.1 %copy-start.1 = (s32[256]{0:T(256)S(1)}, s32[256]{0:T(256)}, u32[]{:S(2)}) copy-start(s32[256]{0:T(256)} %param.15) | copy-start | bytes 3076
  160.9 100.6 %all-to-all-start = ((bf16[2,128,8192]{2,0,1:T(2,128)(2,1)}), bf16[2,128,8192]{2,0,1:T(2,128)(2,1)}, u32[]{:S(2)}, u32[]{:S(2)}) async-start(bf16[2,128,8192]{2,0,1:T(2,128)(2,1)} %copy.10), calls=%async_computation | async-start | bytes 8388608 | tf_op jit(solution)/shard_map/all_to_all | solution.py:22
  165.7 229.9 %reduce-scatter.3.cloned.1.call-start = ((), (), s32[]{:S(2)}) async-start(), calls=%async_computation.7 | async-start | bytes 10485760 | tf_op jit(solution)/shard_map/reduce_scatter | solution.py:42
  199.4 0.7 copy-start.2
  199.4 0.7 copy-start.3
  391.9 124.7 %all-to-all-start.1 = ((bf16[64,4,8192]{2,1,0:T(4,128)(2,1)}), bf16[64,4,8192]{2,1,0:T(4,128)(2,1)}, u32[]{:S(2)}, u32[]{:S(2)}) async-start(bf16[64,4,8192]{2,1,0:T(4,128)(2,1)} %get-tuple-element.5), calls=%async_computation.1 | async-start | bytes 8388608 | tf_op jit(solution)/shard_map/all_to_all | solution.py:30
  395.5 135.2 %reduce-scatter.5.cloned.1.call-start = ((), (), s32[]{:S(2)}) async-start(), calls=%async_computation.8 | async-start | bytes 2359296 | tf_op jit(solution)/shard_map/reduce_scatter | solution.py:43
Sparse Core Ops, SparseCore 0:
  52.4 122.2 all-gather.1
  199.5 77.7 reduce-scatter.2
  399.9 116.0 reduce-scatter.4
where the time goes:
time: 547 us; the launch traced here: 539 us
  waiting for transfers between devices  267 us (49%)
  blocking collectives  126 us (23%)
  local copies, waits for them, and re-layouts  93.1 us (17%)
  starting transfers between devices  16.2 us (3%)
  between operations  14.3 us (3%)
  matrix products  13 us (2%)
  other arithmetic  9.29 us (2%)
    all_to_all x1, waiting for transfers between devices, relocate(): lax.all_to_all(picked[0], ('gx', 'gy'), split_axis=0, concat_axis=1, tile...  106 us
    all_to_all x1, waiting for transfers between devices, relocate(): lax.all_to_all(shaped[1], ('gx', 'gy'), split_axis=1, concat_axis=0, tile...  100 us
    all_to_all x1, blocking collectives, relocate(): lax.all_to_all(picked[1], ('gx', 'gy'), split_axis=0, concat_axis=1, tile...  97.3 us
    all_to_all x1, waiting for transfers between devices, relocate(): lax.all_to_all(shaped[0], ('gx', 'gy'), split_axis=1, concat_axis=0, tile...  51.5 us
    all_gather x1, blocking collectives, shards(): feature_rows = lax.all_gather(tokens, 'gx', axis=1, tiled=True)  29 us
    dot_general x1, matrix products, layer_terms(): return jnp.dot(hidden, down_rows, preferred_element_type=jnp.float32)  13 us
    gather x1, local copies, waits for them, and re-layouts, shards(): ordered = jnp.take(everyone, route, axis=0)  11.7 us
  transfers between devices with their start and end apart: 6, of which 4 were waited for; matrix products, arithmetic and copies ran while one was open for 19% of the time, Pallas kernels for 0%

commit v1 on v0

v1 whole, which is shorter than its diff:
```python
import functools

import jax
import jax.numpy as jnp
from jax import lax
from jax.experimental import pallas as pl
from jax.experimental.pallas import tpu as pltpu
from jax.sharding import PartitionSpec as P


BLOCK = 128
AXES = ("gx", "gy")
CHUNKS = 2
SPARE = 2
STEP = 2


ANY = pl.BlockSpec(memory_space=pl.ANY)
VMEM = pl.BlockSpec(memory_space=pltpu.VMEM)
SMEM = pl.BlockSpec(memory_space=pltpu.SMEM)


def run_all(copies):
    for copy in copies:
        copy.start()
    for copy in copies:
        copy.wait()


def cost(bytes_moved):
    return pl.CostEstimate(flops=bytes_moved * 8, bytes_accessed=bytes_moved, transcendentals=0)


def cut(rows, column, columns):
    held, group, r, _ = rows.shape

    def body(rows_ref, out_ref, sems):
        run_all([
            pltpu.make_async_copy(rows_ref.at[k, :, :, pl.ds(column, columns)], out_ref.at[:, k], sems.at[k])
            for k in range(held)
        ])

    return pl.pallas_call(
        body,
        out_shape=jax.ShapeDtypeStruct((group, held, r, columns), rows.dtype),
        in_specs=[ANY],
        out_specs=VMEM,
        scratch_shapes=[pltpu.SemaphoreType.DMA((held,))],
        cost_estimate=cost(4 * group * held * r * columns),
        name="cut",
    )(rows)


def pick(index, *pools):
    count, tail = index.shape[0], pools[0].shape[1:]

    def body(index_ref, *refs):
        pool_refs, out_ref, sems = refs[: len(pools)], refs[-2], refs[-1]

        def fetch(i, carry):
            at, first = index_ref[i], 0
            for ref in pool_refs:
                size = ref.shape[0]

                @pl.when((at >= first) & (at < first + size))
                def _(ref=ref, first=first):
                    pltpu.make_async_copy(ref.at[at - first], out_ref.at[i], sems.at[i]).start()

                first += size
            return carry

        def settle(i, carry):
            pltpu.make_async_copy(pool_refs[0].at[0], out_ref.at[i], sems.at[i]).wait()
            return carry

        lax.fori_loop(0, count, fetch, 0)
        lax.fori_loop(0, count, settle, 0)

    size = count * tail[0] * tail[1]
    return pl.pallas_call(
        body,
        out_shape=jax.ShapeDtypeStruct((count, *tail), pools[0].dtype),
        in_specs=[SMEM] + [ANY] * len(pools),
        out_specs=VMEM,
        scratch_shapes=[pltpu.SemaphoreType.DMA((count,))],
        cost_estimate=cost(4 * size),
        name="pick",
    )(index, *pools)


def put(landed, column, whole, shape):
    group, held, r, columns = landed.shape

    def body(landed_ref, *refs):
        out_ref, sems = refs[-2], refs[-1]
        run_all([
            pltpu.make_async_copy(landed_ref.at[:, k], out_ref.at[k, :, :, pl.ds(column, columns)], sems.at[k])
            for k in range(held)
        ])

    extra = [] if whole is None else [whole]
    return pl.pallas_call(
        body,
        out_shape=jax.ShapeDtypeStruct(shape, landed.dtype),
        in_specs=[VMEM] + [ANY] * len(extra),
        out_specs=ANY,
        scratch_shapes=[pltpu.SemaphoreType.DMA((held,))],
        input_output_aliases={1: 0} if extra else {},
        cost_estimate=cost(4 * group * held * r * columns),
        name="put",
    )(landed, *extra)


def plan(old_slot, new_owner, hot_rank, held, nx, ny):
    half = ny // 2
    size = nx * half * held

    def place(slot):
        device, k = lax.div(slot, held), lax.rem(slot, held)
        x, y = lax.div(device, ny), lax.rem(device, ny)
        return lax.div(y, half) * size + (x * half + lax.rem(y, half)) * held + k

    target, origin = place(new_owner * held + hot_rank), place(old_slot)
    at = jnp.arange(2 * size, dtype=jnp.int32)
    found = jnp.sum(jnp.where(target[None, :] == at[:, None], origin[None, :], 0), axis=1).reshape(2, size)
    side = jnp.arange(2, dtype=jnp.int32)[:, None]
    crosses = lax.div(found, size) != side
    within = lax.rem(found, size)
    i = jnp.arange(size, dtype=jnp.int32)
    rank = jnp.sum(jnp.where((i[None, :] < i[:, None])[None] & crosses[:, None, :], 1, 0), axis=2)
    land = jnp.where(crosses, size + rank, within)
    taken = (rank[:, None, :] == i[None, :, None]) & crosses[:, None, :]
    send = jnp.sum(jnp.where(taken, within[:, None, :], 0), axis=2)[::-1]
    return send.astype(jnp.int32), land.astype(jnp.int32), jnp.sum(crosses[0].astype(jnp.int32))


def relocate(arrays, old_slot, new_owner, hot_rank, nx, ny):
    half, width = ny // 2, arrays[0].shape[1]
    held = arrays[0].shape[0] // BLOCK
    group = nx * half
    r, size = BLOCK // group, group * held
    fixed = min(size, size // 2 + SPARE)
    columns = width // CHUNKS
    halves = [[x * ny + h * half + y for x in range(nx) for y in range(half)] for h in range(2)]
    across = [(d, d - d % ny + (d % ny + half) % ny) for d in range(nx * ny)]
    side = lax.div(lax.axis_index("gy"), half)

    sends, lands, crossing = plan(old_slot, new_owner, hot_rank, held, nx, ny)
    send = lax.dynamic_index_in_dim(sends, side, keepdims=False)
    land = lax.dynamic_index_in_dim(lands, side, keepdims=False)

    def swap(x):
        return lax.all_to_all(x, AXES, split_axis=0, concat_axis=0, tiled=True, axis_index_groups=halves)

    def spill(own, received):
        def step(i, extra):
            some = pick(lax.dynamic_slice_in_dim(padded, fixed + i * STEP, STEP), own)
            return lax.dynamic_update_slice_in_dim(extra, lax.ppermute(some, AXES, across), i * STEP, 0)

        steps = -(-(size - fixed) // STEP)
        padded = jnp.concatenate([send, jnp.zeros((STEP,), jnp.int32)])
        extra = jnp.zeros((steps * STEP, *own.shape[1:]), own.dtype)
        extra = lax.fori_loop(0, lax.div(crossing - fixed + STEP - 1, STEP), step, extra)
        return pick(land, own, received, extra)

    pieces = [(a, c * columns) for c in range(CHUNKS) for a in range(len(arrays))]
    split = [x.reshape(held, group, r, width) for x in arrays]
    out = [None] * len(arrays)
    count = len(pieces)
    own, received, landed = [None] * count, [None] * count, [None] * count

    def spread(c, *after):
        a, column = pieces[c]
        mine = lax.optimization_barrier((cut(split[a], column, columns), *after))[0]
        own[c] = swap(mine).reshape(size, r, columns)

    def cross(c):
        chosen = pick(send[:fixed], own[c])
        received[c] = lax.ppermute(chosen, AXES, across)
        return chosen

    def gather(c, *after):
        ordered = lax.cond(crossing <= fixed, functools.partial(pick, land), spill, own[c], received[c])
        ordered = lax.optimization_barrier((ordered, *after))[0]
        landed[c] = swap(ordered.reshape(group, held, r, columns))

    spread(0)
    first = cross(0)
    spread(1, own[0], first)
    for c in range(count):
        if c + 1 < count:
            chosen = cross(c + 1)
        if c + 2 < count:
            spread(c + 2, own[c + 1], chosen, *([landed[c - 1]] if c else []))
        gather(c, *([own[c + 2]] if c + 2 < count else []), *([landed[c - 1]] if c else []))
    for c, (a, column) in enumerate(pieces):
        out[a] = put(landed[c], column, out[a], split[a].shape)
    return tuple(x.reshape(held * BLOCK, width) for x in out)


def bits_of(n):
    return [1 << k for k in range(n.bit_length() - 1)]


def reversed_bits(i, n):
    bits = bits_of(n)
    return sum(lax.div(i, b) % 2 * (n // 2 // b) for b in bits) if bits else i


def pairs(axis, n, bit):
    return dict(axis_name=axis, perm=[(i, i ^ bit) for i in range(n)])


def project_up(x, rows, up):
    blocks, (count, feature) = len(rows), rows[0].shape
    hidden = up.shape[0]
    piece = min(feature, 512)

    def body(x_ref, *refs):
        row_refs, up_ref, out_ref = refs[:blocks], refs[blocks], refs[blocks + 1]
        out_ref[...] = jnp.zeros_like(out_ref)
        for j in range(blocks):
            first = (x_ref[0] ^ j) * feature

            def step(i, carry, j=j, first=first):
                at = pl.multiple_of(i * piece, piece)
                out_ref[...] += lax.dot_general(
                    row_refs[j][:, pl.ds(at, piece)],
                    up_ref[:, pl.ds(pl.multiple_of(first + at, piece), piece)],
                    (((1,), (1,)), ((), ())),
                    preferred_element_type=jnp.float32,
                )
                return carry

            lax.fori_loop(0, feature // piece, step, 0)

    return pl.pallas_call(
        body,
        out_shape=jax.ShapeDtypeStruct((count, hidden), jnp.float32),
        in_specs=[SMEM] + [VMEM] * (blocks + 1),
        out_specs=VMEM,
        cost_estimate=cost(4 * blocks * count * feature),
        name="project_up",
    )(x, *rows, up)


def project_down(x, hidden, down, blocks):
    count, feature = hidden.shape[0], down.shape[1] // blocks
    piece = min(feature, 512)

    def body(x_ref, hidden_ref, down_ref, keep_ref, send_ref):
        for j in range(blocks):
            first = (x_ref[0] ^ j) * feature

            def step(i, carry, j=j, first=first):
                at = pl.multiple_of(i * piece, piece)
                part = jnp.dot(
                    hidden_ref[...],
                    down_ref[:, pl.ds(pl.multiple_of(first + at, piece), piece)],
                    preferred_element_type=jnp.float32,
                )
                into = send_ref if j % 2 else keep_ref
                into[j // 2, :, pl.ds(at, piece)] = part
                return carry

            lax.fori_loop(0, feature // piece, step, 0)

    shape = (blocks // 2, count, feature)
    return pl.pallas_call(
        body,
        out_shape=(jax.ShapeDtypeStruct(shape, jnp.float32),) * 2,
        in_specs=[SMEM, VMEM, VMEM],
        out_specs=(VMEM, VMEM),
        cost_estimate=cost(8 * blocks * count * feature),
        name="project_down",
    )(x, hidden, down)


def layer(tokens, up, down, route, nx, ny):
    x, y = lax.axis_index("gx"), lax.axis_index("gy")
    held = tokens.shape[0]

    rows = tokens
    for bit in reversed(bits_of(ny)):
        rows = jnp.concatenate([rows, lax.ppermute(rows, **pairs("gy", ny, bit))])
    every = {0: rows}
    for bit in reversed(bits_of(nx)):
        every |= {j ^ bit: lax.ppermute(part, **pairs("gx", nx, bit)) for j, part in every.items()}

    at = jnp.arange(ny, dtype=jnp.int32)
    wanted = reversed_bits(at, ny) ^ y
    token = jnp.sum(jnp.where(wanted[:, None, None] == at[None, :, None], route.reshape(1, ny, held), 0), axis=1)
    index = (reversed_bits(lax.div(token, held) ^ y, ny) * held + lax.rem(token, held)).reshape(-1)

    own = x.reshape(1).astype(jnp.int32)
    pre = project_up(own, [every[j] for j in range(nx)], up)
    hidden = jax.nn.gelu(pre, approximate=False).astype(jnp.bfloat16)
    hidden = hidden.at[index].get(mode="promise_in_bounds")
    keep, send = project_down(own, hidden, down, nx)
    for bit in bits_of(nx):
        got = lax.ppermute(send, **pairs("gx", nx, bit))
        if 2 * bit < nx:
            send = (keep[1::2] + got[1::2]).astype(jnp.bfloat16)
            keep = keep[::2] + got[::2]
        else:
            total = keep[0] + got[0]
    for bit in bits_of(ny):
        here, there = jnp.split(total, 2)
        total = here + lax.ppermute(there, **pairs("gy", ny, bit))
    return total.astype(jnp.bfloat16)


def solution(mesh):
    nx, ny = mesh.shape["gx"], mesh.shape["gy"]

    def shards(tokens, up_old, down_old, old_slot, new_owner, hot_rank, route):
        mixed = layer(tokens, up_old, down_old, route, nx, ny)
        up_new, down_new = relocate((up_old, down_old), old_slot, new_owner, hot_rank, nx, ny)
        return (up_new, down_new, mixed)

    in_specs = (P("gy", "gx"), P(AXES, None), P(AXES, None), P(), P(), P(), P())
    out_specs = (P(AXES, None), P(AXES, None), P("gy", "gx"))
    return jax.shard_map(shards, mesh=mesh, in_specs=in_specs, out_specs=out_specs, check_vma=False)
```

time: 547 us -> 529 us (0.967); the launches traced: 539 us -> 528 us
  blocking collectives: 126 us -> 0 us
  waiting for transfers between devices: 267 us -> 369 us
  local copies, waits for them, and re-layouts: 93.1 us -> 7.06 us
  Pallas kernels: 0 us -> 76 us
  starting transfers between devices: 16.2 us -> 64.2 us
  matrix products: 13 us -> 0 us
  between operations: 14.3 us -> 1.65 us
    ppermute x0 -> x15, waiting for transfers between devices: none -> 299 us  [the longest x4 188 us: cross(): received[c] = lax.ppermute(chosen, AXES, across)]
    all_to_all x3 -> x8, waiting for transfers between devices: 258 us -> 69.5 us  [swap(): lax.all_to_all(x, AXES, split_axis=0, concat_axis=0, tiled=True, axis_ind...]
    all_to_all x1 -> x0, blocking collectives: 97.3 us -> none  [relocate(): lax.all_to_all(picked[1], ('gx', 'gy'), split_axis=0, concat_axis=1, tile...]
    pallas_call x0 -> x18, Pallas kernels: none -> 76 us  [the longest x8 35.1 us: pick(): pl.pallas_call(body, out_shape=jax.ShapeDtypeStruct((count, *tail), pools...]
    all_to_all x4 -> x0, local copies, waits for them, and re-layouts: 31.4 us -> none  [the longest x1 8.8 us: relocate(): lax.all_to_all(shaped[1], ('gx', 'gy'), split_axis=1, concat_axis=0, tile...]
    reshape x4 -> x1, local copies, waits for them, and re-layouts: 30.9 us -> 0.08 us  [plan(): jnp.sum(jnp.where(target[None, :] == at[:, None], origin[None, :], 0), ax...]
    all_gather x1 -> x0, blocking collectives: 29 us -> none  [shards(): feature_rows = lax.all_gather(tokens, 'gx', axis=1, tiled=True)]
    gather x3 -> x1, local copies, waits for them, and re-layouts: 29.1 us -> 1.81 us  [layer(): hidden = hidden.at[index].get(mode='promise_in_bounds')]
  transfers between devices with their start and end apart: 6 -> 23, of which waited for: 4 -> 15; matrix products, arithmetic and copies ran while one was open for 19% -> 3% of each run, Pallas kernels for 0% -> 12%
where the time goes in v1:
time: 529 us; the launch traced here: 528 us
  waiting for transfers between devices  369 us (70%)
  Pallas kernels  76 us (14%)
  starting transfers between devices  64.2 us (12%)
  other arithmetic  10.2 us (2%)
  local copies, waits for them, and re-layouts  7.06 us (1%)
    ppermute x4, waiting for transfers between devices, cross(): received[c] = lax.ppermute(chosen, AXES, across)  188 us
    all_to_all x8, waiting for transfers between devices, swap(): lax.all_to_all(x, AXES, split_axis=0, concat_axis=0, tiled=True, axis_ind...  69.5 us
    ppermute x3, waiting for transfers between devices, layer(): total = here + lax.ppermute(there, **pairs('gy', ny, bit))  66.6 us
    all_to_all x8, starting transfers between devices, swap(): lax.all_to_all(x, AXES, split_axis=0, concat_axis=0, tiled=True, axis_ind...  41.4 us
    ppermute x3, waiting for transfers between devices, layer(): rows = jnp.concatenate([rows, lax.ppermute(rows, **pairs('gy', ny, bit))])  40.9 us
    pallas_call x8, Pallas kernels, pick(): pl.pallas_call(body, out_shape=jax.ShapeDtypeStruct((count, *tail), pools...  35.1 us
    pallas_call x4, Pallas kernels, put(): pl.pallas_call(body, out_shape=jax.ShapeDtypeStruct(shape, landed.dtype),...  11.7 us
    pallas_call x4, Pallas kernels, cut(): pl.pallas_call(body, out_shape=jax.ShapeDtypeStruct((group, held, r, colu...  11.5 us
  transfers between devices with their start and end apart: 23, of which 15 were waited for; matrix products, arithmetic and copies ran while one was open for 3% of the time, Pallas kernels for 12%

profile of v1, /device:TPU:0, one launch (start us, length us, event | category | flops | bytes accessed | tf_op | source)
XLA Modules:
  0.0 527.9 jit_solution(16195442110725147787)
XLA Ops:
  3.6 6.5 %all-to-all-start = ((bf16[16,2,8,4096]{3,2,1,0:T(8,128)(2,1)}), bf16[16,2,8,4096]{3,2,1,0:T(8,128)(2,1)S(1)}, u32[]{:S(2)}, u32[]{:S(2)}) async-start(bf16[16,2,8,4096]{3,2,1,0:T(8,128)(2,1)} %cut.6), calls=%async_computation | async-start | bytes 4194304 | tf_op jit(solution)/shard_map/all_to_all | solution.py:153
  14.0 23.6 %all-to-all-done = bf16[16,2,8,4096]{3,2,1,0:T(8,128)(2,1)S(1)} async-done(((bf16[16,2,8,4096]{3,2,1,0:T(8,128)(2,1)}), bf16[16,2,8,4096]{3,2,1,0:T(8,128)(2,1)S(1)}, u32[]{:S(2)}, u32[]{:S(2)}) %all-to-all-start) | async-done | bytes 2097184 | tf_op jit(solution)/shard_map/all_to_all | solution.py:153
  48.3 24.7 %all-to-all-done.1 = bf16[16,2,8,4096]{3,2,1,0:T(8,128)(2,1)S(1)} async-done(((bf16[16,2,8,4096]{3,2,1,0:T(8,128)(2,1)}), bf16[16,2,8,4096]{3,2,1,0:T(8,128)(2,1)S(1)}, u32[]{:S(2)}, u32[]{:S(2)}) %all-to-all-start.1) | async-done | bytes 2097184 | tf_op jit(solution)/shard_map/all_to_all | solution.py:153
  85.0 45.9 %collective-permute-done.6 = bf16[18,8,4096]{2,1,0:T(8,128)(2,1)S(1)} collective-permute-done((bf16[18,8,4096]{2,1,0:T(8,128)(2,1)}, bf16[18,8,4096]{2,1,0:T(8,128)(2,1)S(1)}, u32[]{:S(2)}, u32[]{:S(2)}) %collective-permute-start.6) | collective-permute-done | bytes 1179680 | tf_op jit(solution)/shard_map/ppermute | solution.py:179
  130.8 5.0 conditional.6
  130.8 5.0 pick.33
  135.9 9.2 %all-to-all-start.3 = ((bf16[16,2,8,4096]{3,2,1,0:T(8,128)(2,1)}), bf16[16,2,8,4096]{3,2,1,0:T(8,128)(2,1)}, u32[]{:S(2)}, u32[]{:S(2)}) async-start(bf16[16,2,8,4096]{3,2,1,0:T(8,128)(2,1)} %bitcast.41), calls=%async_computation.3 | async-start | bytes 4194304 | tf_op jit(solution)/shard_map/all_to_all | solution.py:153
  151.7 21.1 %all-to-all-done.3.landed_ref = bf16[16,2,8,4096]{3,2,1,0:T(8,128)(2,1)} async-done(((bf16[16,2,8,4096]{3,2,1,0:T(8,128)(2,1)}), bf16[16,2,8,4096]{3,2,1,0:T(8,128)(2,1)}, u32[]{:S(2)}, u32[]{:S(2)}) %all-to-all-start.3) | async-done | bytes 2097184 | tf_op jit(solution)/shard_map/all_to_all | solution.py:153
  180.6 23.7 %collective-permute-done.8 = bf16[32,2048]{1,0:T(8,128)(2,1)S(1)} collective-permute-done((bf16[32,2048]{1,0:T(8,128)(2,1)S(1)}, bf16[32,2048]{1,0:T(8,128)(2,1)S(1)}, u32[]{:S(2)}, u32[]{:S(2)}) %collective-permute-start.8) | collective-permute-done | bytes 131104 | tf_op jit(solution)/shard_map/ppermute | solution.py:285
  204.3 7.6 %collective-permute-start.9 = (bf16[64,2048]{1,0:T(8,128)(2,1)S(1)}, bf16[64,2048]{1,0:T(8,128)(2,1)S(1)}, u32[]{:S(2)}, u32[]{:S(2)}) collective-permute-start(bf16[64,2048]{1,0:T(8,128)(2,1)S(1)} %pad_maximum_fusion.1), channel_id=1, source_target_pairs={{0,2},{1,3},{2,0},{3,1},{4,6},{5,7},{6,4},{7,5},{8,10},{9,11},{10,... | collective-permute-start | bytes 786440 | tf_op jit(solution)/shard_map/ppermute | solution.py:285
  211.9 6.3 %collective-permute-done.9 = bf16[64,2048]{1,0:T(8,128)(2,1)S(1)} collective-permute-done((bf16[64,2048]{1,0:T(8,128)(2,1)S(1)}, bf16[64,2048]{1,0:T(8,128)(2,1)S(1)}, u32[]{:S(2)}, u32[]{:S(2)}) %collective-permute-start.9) | collective-permute-done | bytes 262176 | tf_op jit(solution)/shard_map/ppermute | solution.py:285
  220.6 10.9 %collective-permute-done.10 = bf16[128,2048]{1,0:T(8,128)(2,1)S(1)} collective-permute-done((bf16[128,2048]{1,0:T(8,128)(2,1)S(1)}, bf16[128,2048]{1,0:T(8,128)(2,1)S(1)}, u32[]{:S(2)}, u32[]{:S(2)}) %collective-permute-start.10) | collective-permute-done | bytes 524320 | tf_op jit(solution)/shard_map/ppermute | solution.py:285
  232.3 39.7 %collective-permute-done.5 = bf16[18,8,4096]{2,1,0:T(8,128)(2,1)S(1)} collective-permute-done((bf16[18,8,4096]{2,1,0:T(8,128)(2,1)}, bf16[18,8,4096]{2,1,0:T(8,128)(2,1)S(1)}, u32[]{:S(2)}, u32[]{:S(2)}) %collective-permute-start.5) | collective-permute-done | bytes 1179680 | tf_op jit(solution)/shard_map/ppermute | solution.py:179
  272.0 5.1 conditional.5
  272.0 5.1 pick.31
  286.2 8.5 %project_up.1 = f32[256,256]{1,0:T(8,128)} custom-call(s32[1]{0:T(128)} %bitcast.15.x_ref, bf16[256,2048]{1,0:T(8,128)(2,1)} %constant_dynamic-update-slice_fusion.4.refs_0_, bf16[256,2048]{1,0:T(8,128)(2,1)} %copy-done.4, bf16[256,2048]{1,0:T(8,128)(2,1)} %collective-permute-done.12.refs_2_, bf16[256,2048]{1,0:T(8,128)(2,1)} %collective-permute-done.13.refs_3_, ...), custom_call_target="tpu_custom_call" | custom-call | flops 67108864 | bytes 8388608 | tf_op jit(solution)/shard_map/project_up/pallas_call | solution.py:237
  298.0 9.1 %project_down.1 = (f32[2,256,2048]{2,1,0:T(8,128)}, f32[2,256,2048]{2,1,0:T(8,128)}) custom-call(s32[1]{0:T(128)} %bitcast.15.x_ref, bf16[256,256]{1,0:T(8,128)(2,1)} %gather_fusion, bf16[256,8192]{1,0:T(8,128)(2,1)} %down_ref.1), custom_call_target="tpu_custom_call" | custom-call | flops 134217728 | bytes 16777216 | tf_op jit(solution)/shard_map/project_down/pallas_call | solution.py:269
  307.3 54.6 %collective-permute-done.4 = bf16[18,8,4096]{2,1,0:T(8,128)(2,1)S(1)} collective-permute-done((bf16[18,8,4096]{2,1,0:T(8,128)(2,1)}, bf16[18,8,4096]{2,1,0:T(8,128)(2,1)S(1)}, u32[]{:S(2)}, u32[]{:S(2)}) %collective-permute-start.4) | collective-permute-done | bytes 1179680 | tf_op jit(solution)/shard_map/ppermute | solution.py:179
  361.9 5.6 %conditional.4 = (bf16[32,8,4096]{2,1,0:T(8,128)(2,1)}) conditional(s32[]{:T(128)} %convert_element_type.24, (s32[]{:T(128)}, s32[32]{0:T(128)S(1)}, bf16[32,8,4096]{2,1,0:T(8,128)(2,1)S(1)}, s32[32]{0:T(128)S(1)}, bf16[18,8,4096]{2,1,0:T(8,128)(2,1)S(1)}) %tuple.157, (s32[32]{0:T(128)S(1)}, bf16[32,8,4096]{2,1,0:T(8,128)(2,1)S(1)}, ...), branch_computations={%region_4.7_spmd, %region_7.8_spmd} | conditional | flops 35651600 | bytes 6161098 | solution.py:183
  361.9 5.6 %pick.29 = bf16[32,8,4096]{2,1,0:T(8,128)(2,1)} custom-call(s32[32]{0:T(128)S(1)} %get-tuple-element.325.index_ref, bf16[32,8,4096]{2,1,0:T(8,128)(2,1)S(1)} %get-tuple-element.326.refs_0_, bf16[18,8,4096]{2,1,0:T(8,128)(2,1)S(1)} %get-tuple-element.327.refs_1_), custom_call_target="tpu_custom_call" | custom-call | flops 33554432 | bytes 4194304 | tf_op jit(solution)/shard_map/cond/branch_1_fun/pick/pallas_call | solution.py:80
  381.4 48.1 %collective-permute-done.7 = bf16[18,8,4096]{2,1,0:T(8,128)(2,1)S(1)} collective-permute-done((bf16[18,8,4096]{2,1,0:T(8,128)(2,1)}, bf16[18,8,4096]{2,1,0:T(8,128)(2,1)S(1)}, u32[]{:S(2)}, u32[]{:S(2)}) %collective-permute-start.7) | collective-permute-done | bytes 1179680 | tf_op jit(solution)/shard_map/ppermute | solution.py:179
  445.3 42.9 %collective-permute-done.16 = f32[128,2048]{1,0:T(8,128)S(1)} collective-permute-done((f32[128,2048]{1,0:T(8,128)S(1)}, f32[128,2048]{1,0:T(8,128)S(1)}, u32[]{:S(2)}, u32[]{:S(2)}) %collective-permute-start.16) | collective-permute-done | bytes 1048608 | tf_op jit(solution)/shard_map/ppermute | solution.py:309
  490.0 11.9 %collective-permute-done.17 = f32[64,2048]{1,0:T(8,128)S(1)} collective-permute-done((f32[64,2048]{1,0:T(8,128)S(1)}, f32[64,2048]{1,0:T(8,128)S(1)}, u32[]{:S(2)}, u32[]{:S(2)}) %collective-permute-start.17) | collective-permute-done | bytes 524320 | tf_op jit(solution)/shard_map/ppermute | solution.py:309
  503.8 11.7 %collective-permute-done.18 = f32[32,2048]{1,0:T(8,128)S(1)} collective-permute-done((f32[32,2048]{1,0:T(8,128)S(1)}, f32[32,2048]{1,0:T(8,128)S(1)}, u32[]{:S(2)}, u32[]{:S(2)}) %collective-permute-start.18) | collective-permute-done | bytes 262176 | tf_op jit(solution)/shard_map/ppermute | solution.py:309
  (99 shorter events, 109.4 us)
Async XLA Ops:
  3.6 34.1 %all-to-all-start = ((bf16[16,2,8,4096]{3,2,1,0:T(8,128)(2,1)}), bf16[16,2,8,4096]{3,2,1,0:T(8,128)(2,1)S(1)}, u32[]{:S(2)}, u32[]{:S(2)}) async-start(bf16[16,2,8,4096]{3,2,1,0:T(8,128)(2,1)} %cut.6), calls=%async_computation | async-start | bytes 4194304 | tf_op jit(solution)/shard_map/all_to_all | solution.py:153
  41.5 31.5 %all-to-all-start.1 = ((bf16[16,2,8,4096]{3,2,1,0:T(8,128)(2,1)}), bf16[16,2,8,4096]{3,2,1,0:T(8,128)(2,1)S(1)}, u32[]{:S(2)}, u32[]{:S(2)}) async-start(bf16[16,2,8,4096]{3,2,1,0:T(8,128)(2,1)} %cut.5), calls=%async_computation.1 | async-start | bytes 4194304 | tf_op jit(solution)/shard_map/all_to_all | solution.py:153
  76.7 59.2 %all-to-all-start.2 = ((bf16[16,2,8,4096]{3,2,1,0:T(8,128)(2,1)}), bf16[16,2,8,4096]{3,2,1,0:T(8,128)(2,1)S(1)}, u32[]{:S(2)}, u32[]{:S(2)}) async-start(bf16[16,2,8,4096]{3,2,1,0:T(8,128)(2,1)} %cut.4), calls=%async_computation.2 | async-start | bytes 4194304 | tf_op jit(solution)/shard_map/all_to_all | solution.py:153
  81.1 49.7 %collective-permute-start.6 = (bf16[18,8,4096]{2,1,0:T(8,128)(2,1)}, bf16[18,8,4096]{2,1,0:T(8,128)(2,1)S(1)}, u32[]{:S(2)}, u32[]{:S(2)}) collective-permute-start(bf16[18,8,4096]{2,1,0:T(8,128)(2,1)} %pick.36), channel_id=1, source_target_pairs={{0,4},{1,5},{2,6},{3,7},{4,0},{5,1},{6,2},{7,3},{8,12},{9,13},{10,... | collective-permute-start | bytes 3538952 | tf_op jit(solution)/shard_map/ppermute | solution.py:179
  135.9 36.9 %all-to-all-start.3 = ((bf16[16,2,8,4096]{3,2,1,0:T(8,128)(2,1)}), bf16[16,2,8,4096]{3,2,1,0:T(8,128)(2,1)}, u32[]{:S(2)}, u32[]{:S(2)}) async-start(bf16[16,2,8,4096]{3,2,1,0:T(8,128)(2,1)} %bitcast.41), calls=%async_computation.3 | async-start | bytes 4194304 | tf_op jit(solution)/shard_map/all_to_all | solution.py:153
  151.7 25.6 %copy-start.3 = (bf16[32,2048]{1,0:T(8,128)(2,1)S(1)}, bf16[32,2048]{1,0:T(8,128)(2,1)}, u32[]{:S(2)}) copy-start(bf16[32,2048]{1,0:T(8,128)(2,1)} %param.23) | copy-start | bytes 393220
  172.8 104.3 %all-to-all-start.4 = ((bf16[16,2,8,4096]{3,2,1,0:T(8,128)(2,1)}), bf16[16,2,8,4096]{3,2,1,0:T(8,128)(2,1)}, u32[]{:S(2)}, u32[]{:S(2)}) async-start(bf16[16,2,8,4096]{3,2,1,0:T(8,128)(2,1)} %cut.7), calls=%async_computation.4 | async-start | bytes 4194304 | tf_op jit(solution)/shard_map/all_to_all | solution.py:153
  177.3 27.0 %collective-permute-start.8 = (bf16[32,2048]{1,0:T(8,128)(2,1)S(1)}, bf16[32,2048]{1,0:T(8,128)(2,1)S(1)}, u32[]{:S(2)}, u32[]{:S(2)}) collective-permute-start(bf16[32,2048]{1,0:T(8,128)(2,1)S(1)} %copy-done.3), channel_id=1, source_target_pairs={{0,4},{1,5},{2,6},{3,7},{4,0},{5,1},{6,2},{7,3},{8,12},{9,13},{10,... | collective-permute-start | bytes 393224 | tf_op jit(solution)/shard_map/ppermute | solution.py:285
  204.3 14.0 %collective-permute-start.9 = (bf16[64,2048]{1,0:T(8,128)(2,1)S(1)}, bf16[64,2048]{1,0:T(8,128)(2,1)S(1)}, u32[]{:S(2)}, u32[]{:S(2)}) collective-permute-start(bf16[64,2048]{1,0:T(8,128)(2,1)S(1)} %pad_maximum_fusion.1), channel_id=1, source_target_pairs={{0,2},{1,3},{2,0},{3,1},{4,6},{5,7},{6,4},{7,5},{8,10},{9,11},{10,... | collective-permute-start | bytes 786440 | tf_op jit(solution)/shard_map/ppermute | solution.py:285
  218.3 13.2 %collective-permute-start.10 = (bf16[128,2048]{1,0:T(8,128)(2,1)S(1)}, bf16[128,2048]{1,0:T(8,128)(2,1)S(1)}, u32[]{:S(2)}, u32[]{:S(2)}) collective-permute-start(bf16[128,2048]{1,0:T(8,128)(2,1)S(1)} %pad_maximum_fusion), channel_id=1, source_target_pairs={{0,1},{1,0},{2,3},{3,2},{4,5},{5,4},{6,7},{7,6},{8,9},{9,8},{10,11... | collective-permute-start | bytes 1572872 | tf_op jit(solution)/shard_map/ppermute | solution.py:285
  218.5 53.5 %collective-permute-start.5 = (bf16[18,8,4096]{2,1,0:T(8,128)(2,1)}, bf16[18,8,4096]{2,1,0:T(8,128)(2,1)S(1)}, u32[]{:S(2)}, u32[]{:S(2)}) collective-permute-start(bf16[18,8,4096]{2,1,0:T(8,128)(2,1)} %pick.37), channel_id=1, source_target_pairs={{0,4},{1,5},{2,6},{3,7},{4,0},{5,1},{6,2},{7,3},{8,12},{9,13},{10,... | collective-permute-start | bytes 3538952 | tf_op jit(solution)/shard_map/ppermute | solution.py:179
  232.3 49.5 %collective-permute-start.12 = (bf16[256,2048]{1,0:T(8,128)(2,1)}, bf16[256,2048]{1,0:T(8,128)(2,1)}, u32[]{:S(2)}, u32[]{:S(2)}) collective-permute-start(bf16[256,2048]{1,0:T(8,128)(2,1)} %constant_dynamic-update-slice_fusion.4.refs_0_), channel_id=1, source_target_pairs={{0,16},{8,24},{16,0},{24,8},{1,17},{9,25},{17,1},{25,9},{2,18},{10... | collective-permute-start | bytes 3145736 | tf_op jit(solution)/shard_map/ppermute | solution.py:288
  277.1 90.4 %all-to-all-start.5 = ((bf16[16,2,8,4096]{3,2,1,0:T(8,128)(2,1)}), bf16[16,2,8,4096]{3,2,1,0:T(8,128)(2,1)}, u32[]{:S(2)}, u32[]{:S(2)}) async-start(bf16[16,2,8,4096]{3,2,1,0:T(8,128)(2,1)} %bitcast.42), calls=%async_computation.5 | async-start | bytes 4194304 | tf_op jit(solution)/shard_map/all_to_all | solution.py:153
  281.6 2.9 collective-permute-start.11
  281.9 4.3 collective-permute-start.13
  307.1 68.9 %collective-permute-start.14 = (f32[2,256,2048]{2,1,0:T(8,128)}, f32[2,256,2048]{2,1,0:T(8,128)}, u32[]{:S(2)}, u32[]{:S(2)}) collective-permute-start(f32[2,256,2048]{2,1,0:T(8,128)} %get-tuple-element.396), channel_id=1, source_target_pairs={{0,8},{8,0},{16,24},{24,16},{1,9},{9,1},{17,25},{25,17},{2,10},{10... | collective-permute-start | bytes 12582920 | tf_op jit(solution)/shard_map/ppermute | solution.py:301
  307.3 54.6 %collective-permute-start.4 = (bf16[18,8,4096]{2,1,0:T(8,128)(2,1)}, bf16[18,8,4096]{2,1,0:T(8,128)(2,1)S(1)}, u32[]{:S(2)}, u32[]{:S(2)}) collective-permute-start(bf16[18,8,4096]{2,1,0:T(8,128)(2,1)} %pick.38), channel_id=1, source_target_pairs={{0,4},{1,5},{2,6},{3,7},{4,0},{5,1},{6,2},{7,3},{8,12},{9,13},{10,... | collective-permute-start | bytes 3538952 | tf_op jit(solution)/shard_map/ppermute | solution.py:179
  367.5 67.0 %all-to-all-start.6 = ((bf16[16,2,8,4096]{3,2,1,0:T(8,128)(2,1)}), bf16[16,2,8,4096]{3,2,1,0:T(8,128)(2,1)S(1)}, u32[]{:S(2)}, u32[]{:S(2)}) async-start(bf16[16,2,8,4096]{3,2,1,0:T(8,128)(2,1)} %bitcast.43), calls=%async_computation.6 | async-start | bytes 4194304 | tf_op jit(solution)/shard_map/all_to_all | solution.py:153
  374.7 54.8 %collective-permute-start.7 = (bf16[18,8,4096]{2,1,0:T(8,128)(2,1)}, bf16[18,8,4096]{2,1,0:T(8,128)(2,1)S(1)}, u32[]{:S(2)}, u32[]{:S(2)}) collective-permute-start(bf16[18,8,4096]{2,1,0:T(8,128)(2,1)} %pick.39), channel_id=1, source_target_pairs={{0,4},{1,5},{2,6},{3,7},{4,0},{5,1},{6,2},{7,3},{8,12},{9,13},{10,... | collective-permute-start | bytes 3538952 | tf_op jit(solution)/shard_map/ppermute | solution.py:179
  379.5 60.9 %collective-permute-start.15 = (bf16[1,256,2048]{2,1,0:T(8,128)(2,1)}, bf16[1,256,2048]{2,1,0:T(8,128)(2,1)}, u32[]{:S(2)}, u32[]{:S(2)}) collective-permute-start(bf16[1,256,2048]{2,1,0:T(8,128)(2,1)} %fusion), channel_id=1, source_target_pairs={{0,16},{8,24},{16,0},{24,8},{1,17},{9,25},{17,1},{25,9},{2,18},{10... | collective-permute-start | bytes 3145736 | tf_op jit(solution)/shard_map/ppermute | solution.py:301
  435.9 89.1 %all-to-all-start.7 = ((bf16[16,2,8,4096]{3,2,1,0:T(8,128)(2,1)}), bf16[16,2,8,4096]{3,2,1,0:T(8,128)(2,1)}, u32[]{:S(2)}, u32[]{:S(2)}) async-start(bf16[16,2,8,4096]{3,2,1,0:T(8,128)(2,1)} %bitcast.44), calls=%async_computation.7 | async-start | bytes 4194304 | tf_op jit(solution)/shard_map/all_to_all | solution.py:153
  443.5 44.7 %collective-permute-start.16 = (f32[128,2048]{1,0:T(8,128)S(1)}, f32[128,2048]{1,0:T(8,128)S(1)}, u32[]{:S(2)}, u32[]{:S(2)}) collective-permute-start(f32[128,2048]{1,0:T(8,128)S(1)} %slice_bitcast_fusion), channel_id=1, source_target_pairs={{0,1},{1,0},{2,3},{3,2},{4,5},{5,4},{6,7},{7,6},{8,9},{9,8},{10,11... | collective-permute-start | bytes 3145736 | tf_op jit(solution)/shard_map/ppermute | solution.py:309
  488.5 13.5 %collective-permute-start.17 = (f32[64,2048]{1,0:T(8,128)S(1)}, f32[64,2048]{1,0:T(8,128)S(1)}, u32[]{:S(2)}, u32[]{:S(2)}) collective-permute-start(f32[64,2048]{1,0:T(8,128)S(1)} %split.33), channel_id=1, source_target_pairs={{0,2},{1,3},{2,0},{3,1},{4,6},{5,7},{6,4},{7,5},{8,10},{9,11},{10,... | collective-permute-start | bytes 1572872 | tf_op jit(solution)/shard_map/ppermute | solution.py:309
  502.0 13.5 %collective-permute-start.18 = (f32[32,2048]{1,0:T(8,128)S(1)}, f32[32,2048]{1,0:T(8,128)S(1)}, u32[]{:S(2)}, u32[]{:S(2)}) collective-permute-start(f32[32,2048]{1,0:T(8,128)S(1)} %split.35), channel_id=1, source_target_pairs={{0,4},{1,5},{2,6},{3,7},{4,0},{5,1},{6,2},{7,3},{8,12},{9,13},{10,... | collective-permute-start | bytes 786440 | tf_op jit(solution)/shard_map/ppermute | solution.py:309
  (8 other events, 35.1 us)

commit v2 on v1

--- a/solution.py
+++ b/solution.py
@@ -10,7 +10,8 @@
 
 BLOCK = 128
 AXES = ("gx", "gy")
-CHUNKS = 2
+LANES = 128
+SHORT = 3 / 8
 SPARE = 2
 STEP = 2
 
@@ -140,7 +141,7 @@
     group = nx * half
     r, size = BLOCK // group, group * held
     fixed = min(size, size // 2 + SPARE)
-    columns = width // CHUNKS
+    short = max(LANES, int(width * SHORT) // LANES * LANES)
     halves = [[x * ny + h * half + y for x in range(nx) for y in range(half)] for h in range(2)]
     across = [(d, d - d % ny + (d % ny + half) % ny) for d in range(nx * ny)]
     side = lax.div(lax.axis_index("gy"), half)
@@ -163,14 +164,14 @@
         extra = lax.fori_loop(0, lax.div(crossing - fixed + STEP - 1, STEP), step, extra)
         return pick(land, own, received, extra)
 
-    pieces = [(a, c * columns) for c in range(CHUNKS) for a in range(len(arrays))]
+    pieces = [(0, 0, short), (0, short, width - short), (1, 0, width - short), (1, width - short, short)]
     split = [x.reshape(held, group, r, width) for x in arrays]
     out = [None] * len(arrays)
     count = len(pieces)
     own, received, landed = [None] * count, [None] * count, [None] * count
 
     def spread(c, *after):
-        a, column = pieces[c]
+        a, column, columns = pieces[c]
         mine = lax.optimization_barrier((cut(split[a], column, columns), *after))[0]
         own[c] = swap(mine).reshape(size, r, columns)
 
@@ -182,18 +183,15 @@
     def gather(c, *after):
         ordered = lax.cond(crossing <= fixed, functools.partial(pick, land), spill, own[c], received[c])
         ordered = lax.optimization_barrier((ordered, *after))[0]
-        landed[c] = swap(ordered.reshape(group, held, r, columns))
+        landed[c] = swap(ordered.reshape(group, held, r, -1))
 
     spread(0)
-    first = cross(0)
-    spread(1, own[0], first)
     for c in range(count):
-        if c + 1 < count:
-            chosen = cross(c + 1)
-        if c + 2 < count:
-            spread(c + 2, own[c + 1], chosen, *([landed[c - 1]] if c else []))
-        gather(c, *([own[c + 2]] if c + 2 < count else []), *([landed[c - 1]] if c else []))
-    for c, (a, column) in enumerate(pieces):
+        spread(c, *([own[c - 1]] if c else []))
+        cross(c)
+    for c in range(count):
+        gather(c, *([landed[c - 1]] if c else []))
+    for c, (a, column, _) in enumerate(pieces):
         out[a] = put(landed[c], column, out[a], split[a].shape)
     return tuple(x.reshape(held * BLOCK, width) for x in out)
 

time: 529 us -> 533 us (level)
    ppermute x2, waiting for transfers between devices: 0.01 us -> 43.6 us  [layer(): got = lax.ppermute(send, **pairs('gx', nx, bit))]
    all_to_all x8, waiting for transfers between devices: 69.5 us -> 37.4 us  [swap(): lax.all_to_all(x, AXES, split_axis=0, concat_axis=0, tiled=True, axis_ind...]
    ppermute x3, waiting for transfers between devices: 66.6 us -> 44.1 us  [layer(): total = here + lax.ppermute(there, **pairs('gy', ny, bit))]
    ppermute x3, waiting for transfers between devices: 3.6 us -> 22.4 us  [layer(): lax.ppermute(part, **pairs('gx', nx, bit))]
    ppermute x4, waiting for transfers between devices: 188 us -> 175 us  [cross(): received[c] = lax.ppermute(chosen, AXES, across)]
    ppermute x3, waiting for transfers between devices: 40.9 us -> 47.5 us  [layer(): rows = jnp.concatenate([rows, lax.ppermute(rows, **pairs('gy', ny, bit))])]
  transfers between devices with their start and end apart: 23 -> 23, of which waited for: 15 -> 13; matrix products, arithmetic and copies ran while one was open for 3% -> 3% of each run, Pallas kernels for 12% -> 13%
where the time goes in v2:
time: 533 us; the launch traced here: 532 us
  waiting for transfers between devices  370 us (69%)
  Pallas kernels  72.5 us (14%)
  starting transfers between devices  66.4 us (12%)
  other arithmetic  11.8 us (2%)
  local copies, waits for them, and re-layouts  9.11 us (2%)
    ppermute x4, waiting for transfers between devices, cross(): received[c] = lax.ppermute(chosen, AXES, across)  175 us
    ppermute x3, waiting for transfers between devices, layer(): rows = jnp.concatenate([rows, lax.ppermute(rows, **pairs('gy', ny, bit))])  47.5 us
    ppermute x3, waiting for transfers between devices, layer(): total = here + lax.ppermute(there, **pairs('gy', ny, bit))  44.1 us
    ppermute x2, waiting for transfers between devices, layer(): got = lax.ppermute(send, **pairs('gx', nx, bit))  43.6 us
    all_to_all x8, starting transfers between devices, swap(): lax.all_to_all(x, AXES, split_axis=0, concat_axis=0, tiled=True, axis_ind...  42.4 us
    all_to_all x8, waiting for transfers between devices, swap(): lax.all_to_all(x, AXES, split_axis=0, concat_axis=0, tiled=True, axis_ind...  37.4 us
    pallas_call x8, Pallas kernels, pick(): pl.pallas_call(body, out_shape=jax.ShapeDtypeStruct((count, *tail), pools...  31.7 us
    ppermute x3, waiting for transfers between devices, layer(): lax.ppermute(part, **pairs('gx', nx, bit))  22.4 us
  transfers between devices with their start and end apart: 23, of which 13 were waited for; matrix products, arithmetic and copies ran while one was open for 3% of the time, Pallas kernels for 13%

profile of v2, /device:TPU:0, one launch (start us, length us, event | category | flops | bytes accessed | tf_op | source)
XLA Modules:
  0.0 531.8 jit_solution(3661256403191703742)
XLA Ops:
  3.2 6.3 %all-to-all-start = ((bf16[16,2,8,3072]{3,2,1,0:T(8,128)(2,1)}), bf16[16,2,8,3072]{3,2,1,0:T(8,128)(2,1)S(1)}, u32[]{:S(2)}, u32[]{:S(2)}) async-start(bf16[16,2,8,3072]{3,2,1,0:T(8,128)(2,1)} %cut.5), calls=%async_computation | async-start | bytes 3145728 | tf_op jit(solution)/shard_map/all_to_all | solution.py:154
  12.7 18.7 %all-to-all-done = bf16[16,2,8,3072]{3,2,1,0:T(8,128)(2,1)S(1)} async-done(((bf16[16,2,8,3072]{3,2,1,0:T(8,128)(2,1)}), bf16[16,2,8,3072]{3,2,1,0:T(8,128)(2,1)S(1)}, u32[]{:S(2)}, u32[]{:S(2)}) %all-to-all-start) | async-done | bytes 1572896 | tf_op jit(solution)/shard_map/all_to_all | solution.py:154
  44.4 41.2 %collective-permute-done.5 = bf16[18,8,3072]{2,1,0:T(8,128)(2,1)S(1)} collective-permute-done((bf16[18,8,3072]{2,1,0:T(8,128)(2,1)}, bf16[18,8,3072]{2,1,0:T(8,128)(2,1)S(1)}, u32[]{:S(2)}, u32[]{:S(2)}) %collective-permute-start.5) | collective-permute-done | bytes 884768 | tf_op jit(solution)/shard_map/ppermute | solution.py:180
  85.5 4.5 conditional.5
  85.5 4.5 pick.31
  90.0 9.2 %all-to-all-start.2 = ((bf16[16,2,8,3072]{3,2,1,0:T(8,128)(2,1)}), bf16[16,2,8,3072]{3,2,1,0:T(8,128)(2,1)}, u32[]{:S(2)}, u32[]{:S(2)}) async-start(bf16[16,2,8,3072]{3,2,1,0:T(8,128)(2,1)} %bitcast.43), calls=%async_computation.2 | async-start | bytes 3145728 | tf_op jit(solution)/shard_map/all_to_all | solution.py:154
  102.5 18.7 %all-to-all-done.2.landed_ref = bf16[16,2,8,3072]{3,2,1,0:T(8,128)(2,1)} async-done(((bf16[16,2,8,3072]{3,2,1,0:T(8,128)(2,1)}), bf16[16,2,8,3072]{3,2,1,0:T(8,128)(2,1)}, u32[]{:S(2)}, u32[]{:S(2)}) %all-to-all-start.2) | async-done | bytes 1572896 | tf_op jit(solution)/shard_map/all_to_all | solution.py:154
  128.4 67.7 %collective-permute-done.4 = bf16[18,8,5120]{2,1,0:T(8,128)(2,1)} collective-permute-done((bf16[18,8,5120]{2,1,0:T(8,128)(2,1)}, bf16[18,8,5120]{2,1,0:T(8,128)(2,1)}, u32[]{:S(2)}, u32[]{:S(2)}) %collective-permute-start.4) | collective-permute-done | bytes 1474592 | tf_op jit(solution)/shard_map/ppermute | solution.py:180
  200.3 4.6 all-to-all-start.3
  205.4 32.3 %collective-permute-done.8 = bf16[32,2048]{1,0:T(8,128)(2,1)S(1)} collective-permute-done((bf16[32,2048]{1,0:T(8,128)(2,1)S(1)}, bf16[32,2048]{1,0:T(8,128)(2,1)S(1)}, u32[]{:S(2)}, u32[]{:S(2)}) %collective-permute-start.8) | collective-permute-done | bytes 131104 | tf_op jit(solution)/shard_map/ppermute | solution.py:283
  237.7 4.6 collective-permute-start.9
  242.3 6.0 %collective-permute-done.9 = bf16[64,2048]{1,0:T(8,128)(2,1)S(1)} collective-permute-done((bf16[64,2048]{1,0:T(8,128)(2,1)S(1)}, bf16[64,2048]{1,0:T(8,128)(2,1)S(1)}, u32[]{:S(2)}, u32[]{:S(2)}) %collective-permute-start.9) | collective-permute-done | bytes 262176 | tf_op jit(solution)/shard_map/ppermute | solution.py:283
  252.0 9.2 %collective-permute-done.10 = bf16[128,2048]{1,0:T(8,128)(2,1)S(1)} collective-permute-done((bf16[128,2048]{1,0:T(8,128)(2,1)S(1)}, bf16[128,2048]{1,0:T(8,128)(2,1)S(1)}, u32[]{:S(2)}, u32[]{:S(2)}) %collective-permute-start.10) | collective-permute-done | bytes 524320 | tf_op jit(solution)/shard_map/ppermute | solution.py:283
  263.1 22.4 %collective-permute-done.12.refs_2_ = bf16[256,2048]{1,0:T(8,128)(2,1)} collective-permute-done((bf16[256,2048]{1,0:T(8,128)(2,1)}, bf16[256,2048]{1,0:T(8,128)(2,1)}, u32[]{:S(2)}, u32[]{:S(2)}) %collective-permute-start.12) | collective-permute-done | bytes 1048608 | tf_op jit(solution)/shard_map/ppermute | solution.py:286
  292.9 8.5 %project_up.1 = f32[256,256]{1,0:T(8,128)} custom-call(s32[1]{0:T(128)} %bitcast.15.x_ref, bf16[256,2048]{1,0:T(8,128)(2,1)} %constant_dynamic-update-slice_fusion.4.refs_0_, bf16[256,2048]{1,0:T(8,128)(2,1)} %collective-permute-done.11.refs_1_, bf16[256,2048]{1,0:T(8,128)(2,1)} %collective-permute-done.12.refs_2_, ...), custom_call_target="tpu_custom_call" | custom-call | flops 67108864 | bytes 8388608 | tf_op jit(solution)/shard_map/project_up/pallas_call | solution.py:235
  304.8 9.1 %project_down.1 = (f32[2,256,2048]{2,1,0:T(8,128)}, f32[2,256,2048]{2,1,0:T(8,128)}) custom-call(s32[1]{0:T(128)} %bitcast.15.x_ref, bf16[256,256]{1,0:T(8,128)(2,1)} %gather_fusion, bf16[256,8192]{1,0:T(8,128)(2,1)} %down_ref.1), custom_call_target="tpu_custom_call" | custom-call | flops 134217728 | bytes 16777216 | tf_op jit(solution)/shard_map/project_down/pallas_call | solution.py:267
  319.4 66.3 %collective-permute-done.7 = bf16[18,8,5120]{2,1,0:T(8,128)(2,1)} collective-permute-done((bf16[18,8,5120]{2,1,0:T(8,128)(2,1)}, bf16[18,8,5120]{2,1,0:T(8,128)(2,1)}, u32[]{:S(2)}, u32[]{:S(2)}) %collective-permute-start.7) | collective-permute-done | bytes 1474592 | tf_op jit(solution)/shard_map/ppermute | solution.py:180
  385.8 5.1 conditional.7
  385.8 5.1 pick.35
  405.1 43.6 %collective-permute-done.15 = bf16[1,256,2048]{2,1,0:T(8,128)(2,1)} collective-permute-done((bf16[1,256,2048]{2,1,0:T(8,128)(2,1)}, bf16[1,256,2048]{2,1,0:T(8,128)(2,1)}, u32[]{:S(2)}, u32[]{:S(2)}) %collective-permute-start.15) | collective-permute-done | bytes 1048608 | tf_op jit(solution)/shard_map/ppermute | solution.py:299
  460.0 6.4 %all-to-all-start.7 = ((bf16[16,2,8,3072]{3,2,1,0:T(8,128)(2,1)}), bf16[16,2,8,3072]{3,2,1,0:T(8,128)(2,1)}, u32[]{:S(2)}, u32[]{:S(2)}) async-start(bf16[16,2,8,3072]{3,2,1,0:T(8,128)(2,1)} %bitcast.44), calls=%async_computation.7 | async-start | bytes 3145728 | tf_op jit(solution)/shard_map/all_to_all | solution.py:154
  466.4 26.6 %collective-permute-done.16 = f32[128,2048]{1,0:T(8,128)} collective-permute-done((f32[128,2048]{1,0:T(8,128)}, f32[128,2048]{1,0:T(8,128)}, u32[]{:S(2)}, u32[]{:S(2)}) %collective-permute-start.16) | collective-permute-done | bytes 1048608 | tf_op jit(solution)/shard_map/ppermute | solution.py:307
  499.0 10.4 %collective-permute-done.17 = f32[64,2048]{1,0:T(8,128)S(1)} collective-permute-done((f32[64,2048]{1,0:T(8,128)S(1)}, f32[64,2048]{1,0:T(8,128)S(1)}, u32[]{:S(2)}, u32[]{:S(2)}) %collective-permute-start.17) | collective-permute-done | bytes 524320 | tf_op jit(solution)/shard_map/ppermute | solution.py:307
  514.9 7.1 %collective-permute-done.18 = f32[32,2048]{1,0:T(8,128)S(1)} collective-permute-done((f32[32,2048]{1,0:T(8,128)S(1)}, f32[32,2048]{1,0:T(8,128)S(1)}, u32[]{:S(2)}, u32[]{:S(2)}) %collective-permute-start.18) | collective-permute-done | bytes 262176 | tf_op jit(solution)/shard_map/ppermute | solution.py:307
  (99 shorter events, 110.0 us)
Async XLA Ops:
  3.2 28.2 %all-to-all-start = ((bf16[16,2,8,3072]{3,2,1,0:T(8,128)(2,1)}), bf16[16,2,8,3072]{3,2,1,0:T(8,128)(2,1)S(1)}, u32[]{:S(2)}, u32[]{:S(2)}) async-start(bf16[16,2,8,3072]{3,2,1,0:T(8,128)(2,1)} %cut.5), calls=%async_computation | async-start | bytes 3145728 | tf_op jit(solution)/shard_map/all_to_all | solution.py:154
  32.6 57.5 %all-to-all-start.1 = ((bf16[16,2,8,5120]{3,2,1,0:T(8,128)(2,1)}), bf16[16,2,8,5120]{3,2,1,0:T(8,128)(2,1)S(1)}, u32[]{:S(2)}, u32[]{:S(2)}) async-start(bf16[16,2,8,5120]{3,2,1,0:T(8,128)(2,1)} %cut.4), calls=%async_computation.1 | async-start | bytes 5242880 | tf_op jit(solution)/shard_map/all_to_all | solution.py:154
  40.3 45.2 %collective-permute-start.5 = (bf16[18,8,3072]{2,1,0:T(8,128)(2,1)}, bf16[18,8,3072]{2,1,0:T(8,128)(2,1)S(1)}, u32[]{:S(2)}, u32[]{:S(2)}) collective-permute-start(bf16[18,8,3072]{2,1,0:T(8,128)(2,1)} %pick.37), channel_id=1, source_target_pairs={{0,4},{1,5},{2,6},{3,7},{4,0},{5,1},{6,2},{7,3},{8,12},{9,13},{10,... | collective-permute-start | bytes 2654216 | tf_op jit(solution)/shard_map/ppermute | solution.py:180
  90.0 31.2 %all-to-all-start.2 = ((bf16[16,2,8,3072]{3,2,1,0:T(8,128)(2,1)}), bf16[16,2,8,3072]{3,2,1,0:T(8,128)(2,1)}, u32[]{:S(2)}, u32[]{:S(2)}) async-start(bf16[16,2,8,3072]{3,2,1,0:T(8,128)(2,1)} %bitcast.43), calls=%async_computation.2 | async-start | bytes 3145728 | tf_op jit(solution)/shard_map/all_to_all | solution.py:154
  121.2 79.1 %all-to-all-start.4 = ((bf16[16,2,8,5120]{3,2,1,0:T(8,128)(2,1)}), bf16[16,2,8,5120]{3,2,1,0:T(8,128)(2,1)S(1)}, u32[]{:S(2)}, u32[]{:S(2)}) async-start(bf16[16,2,8,5120]{3,2,1,0:T(8,128)(2,1)} %cut.7), calls=%async_computation.4 | async-start | bytes 5242880 | tf_op jit(solution)/shard_map/all_to_all | solution.py:154
  128.4 67.8 %collective-permute-start.4 = (bf16[18,8,5120]{2,1,0:T(8,128)(2,1)}, bf16[18,8,5120]{2,1,0:T(8,128)(2,1)}, u32[]{:S(2)}, u32[]{:S(2)}) collective-permute-start(bf16[18,8,5120]{2,1,0:T(8,128)(2,1)} %pick.36), channel_id=1, source_target_pairs={{0,4},{1,5},{2,6},{3,7},{4,0},{5,1},{6,2},{7,3},{8,12},{9,13},{10,... | collective-permute-start | bytes 4423688 | tf_op jit(solution)/shard_map/ppermute | solution.py:180
  200.3 88.1 %all-to-all-start.3 = ((bf16[16,2,8,5120]{3,2,1,0:T(8,128)(2,1)}), bf16[16,2,8,5120]{3,2,1,0:T(8,128)(2,1)}, u32[]{:S(2)}, u32[]{:S(2)}) async-start(bf16[16,2,8,5120]{3,2,1,0:T(8,128)(2,1)} %bitcast.41), calls=%async_computation.3 | async-start | bytes 5242880 | tf_op jit(solution)/shard_map/all_to_all | solution.py:154
  205.0 80.6 %copy-start.5 = (s32[256]{0:T(256)S(1)}, s32[256]{0:T(256)}, u32[]{:S(2)}) copy-start(s32[256]{0:T(256)} %param.29) | copy-start | bytes 3076
  205.0 32.7 %collective-permute-start.8 = (bf16[32,2048]{1,0:T(8,128)(2,1)S(1)}, bf16[32,2048]{1,0:T(8,128)(2,1)S(1)}, u32[]{:S(2)}, u32[]{:S(2)}) collective-permute-start(bf16[32,2048]{1,0:T(8,128)(2,1)S(1)} %copy-done.4), channel_id=1, source_target_pairs={{0,4},{1,5},{2,6},{3,7},{4,0},{5,1},{6,2},{7,3},{8,12},{9,13},{10,... | collective-permute-start | bytes 393224 | tf_op jit(solution)/shard_map/ppermute | solution.py:283
  237.7 10.6 %collective-permute-start.9 = (bf16[64,2048]{1,0:T(8,128)(2,1)S(1)}, bf16[64,2048]{1,0:T(8,128)(2,1)S(1)}, u32[]{:S(2)}, u32[]{:S(2)}) collective-permute-start(bf16[64,2048]{1,0:T(8,128)(2,1)S(1)} %pad_maximum_fusion.1), channel_id=1, source_target_pairs={{0,2},{1,3},{2,0},{3,1},{4,6},{5,7},{6,4},{7,5},{8,10},{9,11},{10,... | collective-permute-start | bytes 786440 | tf_op jit(solution)/shard_map/ppermute | solution.py:283
  248.4 12.9 %collective-permute-start.10 = (bf16[128,2048]{1,0:T(8,128)(2,1)S(1)}, bf16[128,2048]{1,0:T(8,128)(2,1)S(1)}, u32[]{:S(2)}, u32[]{:S(2)}) collective-permute-start(bf16[128,2048]{1,0:T(8,128)(2,1)S(1)} %pad_maximum_fusion), channel_id=1, source_target_pairs={{0,1},{1,0},{2,3},{3,2},{4,5},{5,4},{6,7},{7,6},{8,9},{9,8},{10,11... | collective-permute-start | bytes 1572872 | tf_op jit(solution)/shard_map/ppermute | solution.py:283
  262.0 23.5 %collective-permute-start.12 = (bf16[256,2048]{1,0:T(8,128)(2,1)}, bf16[256,2048]{1,0:T(8,128)(2,1)}, u32[]{:S(2)}, u32[]{:S(2)}) collective-permute-start(bf16[256,2048]{1,0:T(8,128)(2,1)} %constant_dynamic-update-slice_fusion.4.refs_0_), channel_id=1, source_target_pairs={{0,16},{8,24},{16,0},{24,8},{1,17},{9,25},{17,1},{25,9},{2,18},{10... | collective-permute-start | bytes 3145736 | tf_op jit(solution)/shard_map/ppermute | solution.py:286
  263.1 29.8 %collective-permute-start.11 = (bf16[256,2048]{1,0:T(8,128)(2,1)}, bf16[256,2048]{1,0:T(8,128)(2,1)}, u32[]{:S(2)}, u32[]{:S(2)}) collective-permute-start(bf16[256,2048]{1,0:T(8,128)(2,1)} %constant_dynamic-update-slice_fusion.4.refs_0_), channel_id=1, source_target_pairs={{0,8},{8,0},{16,24},{24,16},{1,9},{9,1},{17,25},{25,17},{2,10},{10... | collective-permute-start | bytes 3145736 | tf_op jit(solution)/shard_map/ppermute | solution.py:286
  285.5 7.4 %collective-permute-start.13 = (bf16[256,2048]{1,0:T(8,128)(2,1)}, bf16[256,2048]{1,0:T(8,128)(2,1)}, u32[]{:S(2)}, u32[]{:S(2)}) collective-permute-start(bf16[256,2048]{1,0:T(8,128)(2,1)} %collective-permute-done.12.refs_2_), channel_id=1, source_target_pairs={{0,8},{8,0},{16,24},{24,16},{1,9},{9,1},{17,25},{25,17},{2,10},{10... | collective-permute-start | bytes 3145736 | tf_op jit(solution)/shard_map/ppermute | solution.py:286
  288.4 102.5 %all-to-all-start.5 = ((bf16[16,2,8,3072]{3,2,1,0:T(8,128)(2,1)}), bf16[16,2,8,3072]{3,2,1,0:T(8,128)(2,1)}, u32[]{:S(2)}, u32[]{:S(2)}) async-start(bf16[16,2,8,3072]{3,2,1,0:T(8,128)(2,1)} %cut.6), calls=%async_computation.5 | async-start | bytes 3145728 | tf_op jit(solution)/shard_map/all_to_all | solution.py:154
  313.9 81.0 %collective-permute-start.14 = (f32[2,256,2048]{2,1,0:T(8,128)}, f32[2,256,2048]{2,1,0:T(8,128)}, u32[]{:S(2)}, u32[]{:S(2)}) collective-permute-start(f32[2,256,2048]{2,1,0:T(8,128)} %get-tuple-element.394), channel_id=1, source_target_pairs={{0,8},{8,0},{16,24},{24,16},{1,9},{9,1},{17,25},{25,17},{2,10},{10... | collective-permute-start | bytes 12582920 | tf_op jit(solution)/shard_map/ppermute | solution.py:299
  318.4 67.3 %collective-permute-start.7 = (bf16[18,8,5120]{2,1,0:T(8,128)(2,1)}, bf16[18,8,5120]{2,1,0:T(8,128)(2,1)}, u32[]{:S(2)}, u32[]{:S(2)}) collective-permute-start(bf16[18,8,5120]{2,1,0:T(8,128)(2,1)} %pick.39), channel_id=1, source_target_pairs={{0,4},{1,5},{2,6},{3,7},{4,0},{5,1},{6,2},{7,3},{8,12},{9,13},{10,... | collective-permute-start | bytes 4423688 | tf_op jit(solution)/shard_map/ppermute | solution.py:180
  390.9 69.1 %all-to-all-start.6 = ((bf16[16,2,8,5120]{3,2,1,0:T(8,128)(2,1)}), bf16[16,2,8,5120]{3,2,1,0:T(8,128)(2,1)S(1)}, u32[]{:S(2)}, u32[]{:S(2)}) async-start(bf16[16,2,8,5120]{3,2,1,0:T(8,128)(2,1)} %bitcast.42), calls=%async_computation.6 | async-start | bytes 5242880 | tf_op jit(solution)/shard_map/all_to_all | solution.py:154
  398.4 50.3 %collective-permute-start.15 = (bf16[1,256,2048]{2,1,0:T(8,128)(2,1)}, bf16[1,256,2048]{2,1,0:T(8,128)(2,1)}, u32[]{:S(2)}, u32[]{:S(2)}) collective-permute-start(bf16[1,256,2048]{2,1,0:T(8,128)(2,1)} %fusion), channel_id=1, source_target_pairs={{0,16},{8,24},{16,0},{24,8},{1,17},{9,25},{17,1},{25,9},{2,18},{10... | collective-permute-start | bytes 3145736 | tf_op jit(solution)/shard_map/ppermute | solution.py:299
  403.2 52.3 %collective-permute-start.6 = (bf16[18,8,3072]{2,1,0:T(8,128)(2,1)}, bf16[18,8,3072]{2,1,0:T(8,128)(2,1)S(1)}, u32[]{:S(2)}, u32[]{:S(2)}) collective-permute-start(bf16[18,8,3072]{2,1,0:T(8,128)(2,1)} %pick.38), channel_id=1, source_target_pairs={{0,4},{1,5},{2,6},{3,7},{4,0},{5,1},{6,2},{7,3},{8,12},{9,13},{10,... | collective-permute-start | bytes 2654216 | tf_op jit(solution)/shard_map/ppermute | solution.py:180
  454.1 39.0 %collective-permute-start.16 = (f32[128,2048]{1,0:T(8,128)}, f32[128,2048]{1,0:T(8,128)}, u32[]{:S(2)}, u32[]{:S(2)}) collective-permute-start(f32[128,2048]{1,0:T(8,128)} %slice_bitcast_fusion), channel_id=1, source_target_pairs={{0,1},{1,0},{2,3},{3,2},{4,5},{5,4},{6,7},{7,6},{8,9},{9,8},{10,11... | collective-permute-start | bytes 3145736 | tf_op jit(solution)/shard_map/ppermute | solution.py:307
  460.0 69.2 %all-to-all-start.7 = ((bf16[16,2,8,3072]{3,2,1,0:T(8,128)(2,1)}), bf16[16,2,8,3072]{3,2,1,0:T(8,128)(2,1)}, u32[]{:S(2)}, u32[]{:S(2)}) async-start(bf16[16,2,8,3072]{3,2,1,0:T(8,128)(2,1)} %bitcast.44), calls=%async_computation.7 | async-start | bytes 3145728 | tf_op jit(solution)/shard_map/all_to_all | solution.py:154
  494.8 14.6 %collective-permute-start.17 = (f32[64,2048]{1,0:T(8,128)S(1)}, f32[64,2048]{1,0:T(8,128)S(1)}, u32[]{:S(2)}, u32[]{:S(2)}) collective-permute-start(f32[64,2048]{1,0:T(8,128)S(1)} %split.33), channel_id=1, source_target_pairs={{0,2},{1,3},{2,0},{3,1},{4,6},{5,7},{6,4},{7,5},{8,10},{9,11},{10,... | collective-permute-start | bytes 1572872 | tf_op jit(solution)/shard_map/ppermute | solution.py:307
  509.5 12.5 %collective-permute-start.18 = (f32[32,2048]{1,0:T(8,128)S(1)}, f32[32,2048]{1,0:T(8,128)S(1)}, u32[]{:S(2)}, u32[]{:S(2)}) collective-permute-start(f32[32,2048]{1,0:T(8,128)S(1)} %split.35), channel_id=1, source_target_pairs={{0,4},{1,5},{2,6},{3,7},{4,0},{5,1},{6,2},{7,3},{8,12},{9,13},{10,... | collective-permute-start | bytes 786440 | tf_op jit(solution)/shard_map/ppermute | solution.py:307
  (8 other events, 69.0 us)

commit v3 on v2

--- a/solution.py
+++ b/solution.py
@@ -11,7 +11,8 @@
 BLOCK = 128
 AXES = ("gx", "gy")
 LANES = 128
-SHORT = 3 / 8
+FIRST = 7 / 16
+LAST = 3 / 8
 SPARE = 2
 STEP = 2
 
@@ -141,7 +142,6 @@
     group = nx * half
     r, size = BLOCK // group, group * held
     fixed = min(size, size // 2 + SPARE)
-    short = max(LANES, int(width * SHORT) // LANES * LANES)
     halves = [[x * ny + h * half + y for x in range(nx) for y in range(half)] for h in range(2)]
     across = [(d, d - d % ny + (d % ny + half) % ny) for d in range(nx * ny)]
     side = lax.div(lax.axis_index("gy"), half)
@@ -164,7 +164,8 @@
         extra = lax.fori_loop(0, lax.div(crossing - fixed + STEP - 1, STEP), step, extra)
         return pick(land, own, received, extra)
 
-    pieces = [(0, 0, short), (0, short, width - short), (1, 0, width - short), (1, width - short, short)]
+    first, last = (max(LANES, int(width * part) // LANES * LANES) for part in (FIRST, LAST))
+    pieces = [(0, 0, first), (0, first, width - first), (1, 0, width - last), (1, width - last, last)]
     split = [x.reshape(held, group, r, width) for x in arrays]
     out = [None] * len(arrays)
     count = len(pieces)
@@ -304,6 +305,8 @@
             total = keep[0] + got[0]
     for bit in bits_of(ny):
         here, there = jnp.split(total, 2)
+        if bit >= ny // 4:
+            there = there.astype(jnp.bfloat16)
         total = here + lax.ppermute(there, **pairs("gy", ny, bit))
     return total.astype(jnp.bfloat16)
 

time: 533 us -> 539 us (1.011)
  waiting for transfers between devices: 370 us -> 376 us
    ppermute x4, waiting for transfers between devices: 175 us -> 168 us  [cross(): received[c] = lax.ppermute(chosen, AXES, across)]
    ppermute x3, waiting for transfers between devices: 22.4 us -> 29.1 us  [layer(): lax.ppermute(part, **pairs('gx', nx, bit))]
    all_to_all x8, waiting for transfers between devices: 37.4 us -> 43.2 us  [swap(): lax.all_to_all(x, AXES, split_axis=0, concat_axis=0, tiled=True, axis_ind...]
  transfers between devices with their start and end apart: 23 -> 23, of which waited for: 13 -> 14; matrix products, arithmetic and copies ran while one was open for 3% -> 3% of each run, Pallas kernels for 13% -> 13%
where the time goes in v3:
time: 539 us; the launch traced here: 537 us
  waiting for transfers between devices  376 us (70%)
  Pallas kernels  72.6 us (13%)
  starting transfers between devices  67.2 us (12%)
  other arithmetic  11.7 us (2%)
  local copies, waits for them, and re-layouts  8.27 us (2%)
    ppermute x4, waiting for transfers between devices, cross(): received[c] = lax.ppermute(chosen, AXES, across)  168 us
    ppermute x3, waiting for transfers between devices, layer(): total = here + lax.ppermute(there, **pairs('gy', ny, bit))  47.9 us
    ppermute x2, waiting for transfers between devices, layer(): got = lax.ppermute(send, **pairs('gx', nx, bit))  44.5 us
    all_to_all x8, waiting for transfers between devices, swap(): lax.all_to_all(x, AXES, split_axis=0, concat_axis=0, tiled=True, axis_ind...  43.2 us
    ppermute x3, waiting for transfers between devices, layer(): rows = jnp.concatenate([rows, lax.ppermute(rows, **pairs('gy', ny, bit))])  43 us
    all_to_all x8, starting transfers between devices, swap(): lax.all_to_all(x, AXES, split_axis=0, concat_axis=0, tiled=True, axis_ind...  42.8 us
    pallas_call x8, Pallas kernels, pick(): pl.pallas_call(body, out_shape=jax.ShapeDtypeStruct((count, *tail), pools...  31.9 us
    ppermute x3, waiting for transfers between devices, layer(): lax.ppermute(part, **pairs('gx', nx, bit))  29.1 us
  transfers between devices with their start and end apart: 23, of which 14 were waited for; matrix products, arithmetic and copies ran while one was open for 3% of the time, Pallas kernels for 13%

profile of v3, /device:TPU:0, one launch (start us, length us, event | category | flops | bytes accessed | tf_op | source)
XLA Modules:
  0.0 537.1 jit_solution(12322936140974930670)
XLA Ops:
  3.3 6.3 %all-to-all-start = ((bf16[16,2,8,3584]{3,2,1,0:T(8,128)(2,1)}), bf16[16,2,8,3584]{3,2,1,0:T(8,128)(2,1)S(1)}, u32[]{:S(2)}, u32[]{:S(2)}) async-start(bf16[16,2,8,3584]{3,2,1,0:T(8,128)(2,1)} %cut.5), calls=%async_computation | async-start | bytes 3670016 | tf_op jit(solution)/shard_map/all_to_all | solution.py:154
  12.7 21.7 %all-to-all-done = bf16[16,2,8,3584]{3,2,1,0:T(8,128)(2,1)S(1)} async-done(((bf16[16,2,8,3584]{3,2,1,0:T(8,128)(2,1)}), bf16[16,2,8,3584]{3,2,1,0:T(8,128)(2,1)S(1)}, u32[]{:S(2)}, u32[]{:S(2)}) %all-to-all-start) | async-done | bytes 1835040 | tf_op jit(solution)/shard_map/all_to_all | solution.py:154
  47.6 41.2 %collective-permute-done.5 = bf16[18,8,3584]{2,1,0:T(8,128)(2,1)S(1)} collective-permute-done((bf16[18,8,3584]{2,1,0:T(8,128)(2,1)}, bf16[18,8,3584]{2,1,0:T(8,128)(2,1)S(1)}, u32[]{:S(2)}, u32[]{:S(2)}) %collective-permute-start.5) | collective-permute-done | bytes 1032224 | tf_op jit(solution)/shard_map/ppermute | solution.py:181
  88.8 4.8 conditional.5
  88.8 4.8 pick.31
  93.7 9.0 %all-to-all-start.2 = ((bf16[16,2,8,3584]{3,2,1,0:T(8,128)(2,1)}), bf16[16,2,8,3584]{3,2,1,0:T(8,128)(2,1)}, u32[]{:S(2)}, u32[]{:S(2)}) async-start(bf16[16,2,8,3584]{3,2,1,0:T(8,128)(2,1)} %bitcast.43), calls=%async_computation.2 | async-start | bytes 3670016 | tf_op jit(solution)/shard_map/all_to_all | solution.py:154
  105.9 21.6 %all-to-all-done.2.landed_ref = bf16[16,2,8,3584]{3,2,1,0:T(8,128)(2,1)} async-done(((bf16[16,2,8,3584]{3,2,1,0:T(8,128)(2,1)}), bf16[16,2,8,3584]{3,2,1,0:T(8,128)(2,1)}, u32[]{:S(2)}, u32[]{:S(2)}) %all-to-all-start.2) | async-done | bytes 1835040 | tf_op jit(solution)/shard_map/all_to_all | solution.py:154
  136.2 59.3 %collective-permute-done.4 = bf16[18,8,4608]{2,1,0:T(8,128)(2,1)} collective-permute-done((bf16[18,8,4608]{2,1,0:T(8,128)(2,1)}, bf16[18,8,4608]{2,1,0:T(8,128)(2,1)}, u32[]{:S(2)}, u32[]{:S(2)}) %collective-permute-start.4) | collective-permute-done | bytes 1327136 | tf_op jit(solution)/shard_map/ppermute | solution.py:181
  199.6 4.6 all-to-all-start.3
  206.5 27.8 %collective-permute-done.8 = bf16[32,2048]{1,0:T(8,128)(2,1)S(1)} collective-permute-done((bf16[32,2048]{1,0:T(8,128)(2,1)S(1)}, bf16[32,2048]{1,0:T(8,128)(2,1)S(1)}, u32[]{:S(2)}, u32[]{:S(2)}) %collective-permute-start.8) | collective-permute-done | bytes 131104 | tf_op jit(solution)/shard_map/ppermute | solution.py:284
  234.3 5.9 %collective-permute-start.9 = (bf16[64,2048]{1,0:T(8,128)(2,1)S(1)}, bf16[64,2048]{1,0:T(8,128)(2,1)S(1)}, u32[]{:S(2)}, u32[]{:S(2)}) collective-permute-start(bf16[64,2048]{1,0:T(8,128)(2,1)S(1)} %pad_maximum_fusion.1), channel_id=1, source_target_pairs={{0,2},{1,3},{2,0},{3,1},{4,6},{5,7},{6,4},{7,5},{8,10},{9,11},{10,... | collective-permute-start | bytes 786440 | tf_op jit(solution)/shard_map/ppermute | solution.py:284
  240.2 6.0 %collective-permute-done.9 = bf16[64,2048]{1,0:T(8,128)(2,1)S(1)} collective-permute-done((bf16[64,2048]{1,0:T(8,128)(2,1)S(1)}, bf16[64,2048]{1,0:T(8,128)(2,1)S(1)}, u32[]{:S(2)}, u32[]{:S(2)}) %collective-permute-start.9) | collective-permute-done | bytes 262176 | tf_op jit(solution)/shard_map/ppermute | solution.py:284
  249.8 9.2 %collective-permute-done.10 = bf16[128,2048]{1,0:T(8,128)(2,1)S(1)} collective-permute-done((bf16[128,2048]{1,0:T(8,128)(2,1)S(1)}, bf16[128,2048]{1,0:T(8,128)(2,1)S(1)}, u32[]{:S(2)}, u32[]{:S(2)}) %collective-permute-start.10) | collective-permute-done | bytes 524320 | tf_op jit(solution)/shard_map/ppermute | solution.py:284
  268.2 26.5 %collective-permute-done.12.refs_2_ = bf16[256,2048]{1,0:T(8,128)(2,1)} collective-permute-done((bf16[256,2048]{1,0:T(8,128)(2,1)}, bf16[256,2048]{1,0:T(8,128)(2,1)}, u32[]{:S(2)}, u32[]{:S(2)}) %collective-permute-start.12) | collective-permute-done | bytes 1048608 | tf_op jit(solution)/shard_map/ppermute | solution.py:287
  297.7 8.4 %project_up.1 = f32[256,256]{1,0:T(8,128)} custom-call(s32[1]{0:T(128)} %bitcast.15.x_ref, bf16[256,2048]{1,0:T(8,128)(2,1)} %constant_dynamic-update-slice_fusion.4.refs_0_, bf16[256,2048]{1,0:T(8,128)(2,1)} %collective-permute-done.11.refs_1_, bf16[256,2048]{1,0:T(8,128)(2,1)} %collective-permute-done.12.refs_2_, ...), custom_call_target="tpu_custom_call" | custom-call | flops 67108864 | bytes 8388608 | tf_op jit(solution)/shard_map/project_up/pallas_call | solution.py:236
  309.4 9.1 %project_down.1 = (f32[2,256,2048]{2,1,0:T(8,128)}, f32[2,256,2048]{2,1,0:T(8,128)}) custom-call(s32[1]{0:T(128)} %bitcast.15.x_ref, bf16[256,256]{1,0:T(8,128)(2,1)} %gather_fusion, bf16[256,8192]{1,0:T(8,128)(2,1)} %down_ref.1), custom_call_target="tpu_custom_call" | custom-call | flops 134217728 | bytes 16777216 | tf_op jit(solution)/shard_map/project_down/pallas_call | solution.py:268
  323.1 67.3 %collective-permute-done.7 = bf16[18,8,5120]{2,1,0:T(8,128)(2,1)} collective-permute-done((bf16[18,8,5120]{2,1,0:T(8,128)(2,1)}, bf16[18,8,5120]{2,1,0:T(8,128)(2,1)}, u32[]{:S(2)}, u32[]{:S(2)}) %collective-permute-start.7) | collective-permute-done | bytes 1474592 | tf_op jit(solution)/shard_map/ppermute | solution.py:181
  390.3 5.1 conditional.7
  390.3 5.1 pick.35
  408.4 44.5 %collective-permute-done.15 = bf16[1,256,2048]{2,1,0:T(8,128)(2,1)} collective-permute-done((bf16[1,256,2048]{2,1,0:T(8,128)(2,1)}, bf16[1,256,2048]{2,1,0:T(8,128)(2,1)}, u32[]{:S(2)}, u32[]{:S(2)}) %collective-permute-start.15) | collective-permute-done | bytes 1048608 | tf_op jit(solution)/shard_map/ppermute | solution.py:300
  452.9 4.5 fusion.1
  461.9 7.3 %all-to-all-start.7 = ((bf16[16,2,8,3072]{3,2,1,0:T(8,128)(2,1)}), bf16[16,2,8,3072]{3,2,1,0:T(8,128)(2,1)}, u32[]{:S(2)}, u32[]{:S(2)}) async-start(bf16[16,2,8,3072]{3,2,1,0:T(8,128)(2,1)} %bitcast.44), calls=%async_computation.7 | async-start | bytes 3145728 | tf_op jit(solution)/shard_map/all_to_all | solution.py:154
  472.6 39.0 %collective-permute-done.16 = f32[128,2048]{1,0:T(8,128)S(1)} collective-permute-done((f32[128,2048]{1,0:T(8,128)S(1)}, f32[128,2048]{1,0:T(8,128)S(1)}, u32[]{:S(2)}, u32[]{:S(2)}) %collective-permute-start.16) | collective-permute-done | bytes 1048608 | tf_op jit(solution)/shard_map/ppermute | solution.py:310
  513.3 6.3 %collective-permute-done.17 = bf16[64,2048]{1,0:T(8,128)(2,1)S(1)} collective-permute-done((bf16[64,2048]{1,0:T(8,128)(2,1)S(1)}, bf16[64,2048]{1,0:T(8,128)(2,1)S(1)}, u32[]{:S(2)}, u32[]{:S(2)}) %collective-permute-start.17) | collective-permute-done | bytes 262176 | tf_op jit(solution)/shard_map/ppermute | solution.py:310
  (99 shorter events, 108.6 us)
Async XLA Ops:
  3.3 31.1 %all-to-all-start = ((bf16[16,2,8,3584]{3,2,1,0:T(8,128)(2,1)}), bf16[16,2,8,3584]{3,2,1,0:T(8,128)(2,1)S(1)}, u32[]{:S(2)}, u32[]{:S(2)}) async-start(bf16[16,2,8,3584]{3,2,1,0:T(8,128)(2,1)} %cut.5), calls=%async_computation | async-start | bytes 3670016 | tf_op jit(solution)/shard_map/all_to_all | solution.py:154
  35.6 58.0 %all-to-all-start.1 = ((bf16[16,2,8,4608]{3,2,1,0:T(8,128)(2,1)}), bf16[16,2,8,4608]{3,2,1,0:T(8,128)(2,1)S(1)}, u32[]{:S(2)}, u32[]{:S(2)}) async-start(bf16[16,2,8,4608]{3,2,1,0:T(8,128)(2,1)} %cut.4), calls=%async_computation.1 | async-start | bytes 4718592 | tf_op jit(solution)/shard_map/all_to_all | solution.py:154
  43.6 45.3 %collective-permute-start.5 = (bf16[18,8,3584]{2,1,0:T(8,128)(2,1)}, bf16[18,8,3584]{2,1,0:T(8,128)(2,1)S(1)}, u32[]{:S(2)}, u32[]{:S(2)}) collective-permute-start(bf16[18,8,3584]{2,1,0:T(8,128)(2,1)} %pick.37), channel_id=1, source_target_pairs={{0,4},{1,5},{2,6},{3,7},{4,0},{5,1},{6,2},{7,3},{8,12},{9,13},{10,... | collective-permute-start | bytes 3096584 | tf_op jit(solution)/shard_map/ppermute | solution.py:181
  93.7 33.8 %all-to-all-start.2 = ((bf16[16,2,8,3584]{3,2,1,0:T(8,128)(2,1)}), bf16[16,2,8,3584]{3,2,1,0:T(8,128)(2,1)}, u32[]{:S(2)}, u32[]{:S(2)}) async-start(bf16[16,2,8,3584]{3,2,1,0:T(8,128)(2,1)} %bitcast.43), calls=%async_computation.2 | async-start | bytes 3670016 | tf_op jit(solution)/shard_map/all_to_all | solution.py:154
  127.4 72.1 %all-to-all-start.4 = ((bf16[16,2,8,5120]{3,2,1,0:T(8,128)(2,1)}), bf16[16,2,8,5120]{3,2,1,0:T(8,128)(2,1)S(1)}, u32[]{:S(2)}, u32[]{:S(2)}) async-start(bf16[16,2,8,5120]{3,2,1,0:T(8,128)(2,1)} %cut.7), calls=%async_computation.4 | async-start | bytes 5242880 | tf_op jit(solution)/shard_map/all_to_all | solution.py:154
  134.5 61.0 %collective-permute-start.4 = (bf16[18,8,4608]{2,1,0:T(8,128)(2,1)}, bf16[18,8,4608]{2,1,0:T(8,128)(2,1)}, u32[]{:S(2)}, u32[]{:S(2)}) collective-permute-start(bf16[18,8,4608]{2,1,0:T(8,128)(2,1)} %pick.36), channel_id=1, source_target_pairs={{0,4},{1,5},{2,6},{3,7},{4,0},{5,1},{6,2},{7,3},{8,12},{9,13},{10,... | collective-permute-start | bytes 3981320 | tf_op jit(solution)/shard_map/ppermute | solution.py:181
  199.6 64.0 %all-to-all-start.3 = ((bf16[16,2,8,4608]{3,2,1,0:T(8,128)(2,1)}), bf16[16,2,8,4608]{3,2,1,0:T(8,128)(2,1)}, u32[]{:S(2)}, u32[]{:S(2)}) async-start(bf16[16,2,8,4608]{3,2,1,0:T(8,128)(2,1)} %bitcast.42), calls=%async_computation.3 | async-start | bytes 4718592 | tf_op jit(solution)/shard_map/all_to_all | solution.py:154
  204.2 30.1 %collective-permute-start.8 = (bf16[32,2048]{1,0:T(8,128)(2,1)S(1)}, bf16[32,2048]{1,0:T(8,128)(2,1)S(1)}, u32[]{:S(2)}, u32[]{:S(2)}) collective-permute-start(bf16[32,2048]{1,0:T(8,128)(2,1)S(1)} %copy-done.4), channel_id=1, source_target_pairs={{0,4},{1,5},{2,6},{3,7},{4,0},{5,1},{6,2},{7,3},{8,12},{9,13},{10,... | collective-permute-start | bytes 393224 | tf_op jit(solution)/shard_map/ppermute | solution.py:284
  234.3 11.9 %collective-permute-start.9 = (bf16[64,2048]{1,0:T(8,128)(2,1)S(1)}, bf16[64,2048]{1,0:T(8,128)(2,1)S(1)}, u32[]{:S(2)}, u32[]{:S(2)}) collective-permute-start(bf16[64,2048]{1,0:T(8,128)(2,1)S(1)} %pad_maximum_fusion.1), channel_id=1, source_target_pairs={{0,2},{1,3},{2,0},{3,1},{4,6},{5,7},{6,4},{7,5},{8,10},{9,11},{10,... | collective-permute-start | bytes 786440 | tf_op jit(solution)/shard_map/ppermute | solution.py:284
  246.2 12.9 %collective-permute-start.10 = (bf16[128,2048]{1,0:T(8,128)(2,1)S(1)}, bf16[128,2048]{1,0:T(8,128)(2,1)S(1)}, u32[]{:S(2)}, u32[]{:S(2)}) collective-permute-start(bf16[128,2048]{1,0:T(8,128)(2,1)S(1)} %pad_maximum_fusion), channel_id=1, source_target_pairs={{0,1},{1,0},{2,3},{3,2},{4,5},{5,4},{6,7},{7,6},{8,9},{9,8},{10,11... | collective-permute-start | bytes 1572872 | tf_op jit(solution)/shard_map/ppermute | solution.py:284
  259.9 34.8 %collective-permute-start.12 = (bf16[256,2048]{1,0:T(8,128)(2,1)}, bf16[256,2048]{1,0:T(8,128)(2,1)}, u32[]{:S(2)}, u32[]{:S(2)}) collective-permute-start(bf16[256,2048]{1,0:T(8,128)(2,1)} %constant_dynamic-update-slice_fusion.4.refs_0_), channel_id=1, source_target_pairs={{0,16},{8,24},{16,0},{24,8},{1,17},{9,25},{17,1},{25,9},{2,18},{10... | collective-permute-start | bytes 3145736 | tf_op jit(solution)/shard_map/ppermute | solution.py:287
  263.5 131.9 %all-to-all-start.5 = ((bf16[16,2,8,3072]{3,2,1,0:T(8,128)(2,1)}), bf16[16,2,8,3072]{3,2,1,0:T(8,128)(2,1)}, u32[]{:S(2)}, u32[]{:S(2)}) async-start(bf16[16,2,8,3072]{3,2,1,0:T(8,128)(2,1)} %cut.6), calls=%async_computation.5 | async-start | bytes 3145728 | tf_op jit(solution)/shard_map/all_to_all | solution.py:154
  268.0 27.1 %collective-permute-start.11 = (bf16[256,2048]{1,0:T(8,128)(2,1)}, bf16[256,2048]{1,0:T(8,128)(2,1)}, u32[]{:S(2)}, u32[]{:S(2)}) collective-permute-start(bf16[256,2048]{1,0:T(8,128)(2,1)} %constant_dynamic-update-slice_fusion.4.refs_0_), channel_id=1, source_target_pairs={{0,8},{8,0},{16,24},{24,16},{1,9},{9,1},{17,25},{25,17},{2,10},{10... | collective-permute-start | bytes 3145736 | tf_op jit(solution)/shard_map/ppermute | solution.py:287
  294.7 3.0 collective-permute-start.13
  318.5 80.7 %collective-permute-start.14 = (f32[2,256,2048]{2,1,0:T(8,128)}, f32[2,256,2048]{2,1,0:T(8,128)}, u32[]{:S(2)}, u32[]{:S(2)}) collective-permute-start(f32[2,256,2048]{2,1,0:T(8,128)} %get-tuple-element.394), channel_id=1, source_target_pairs={{0,8},{8,0},{16,24},{24,16},{1,9},{9,1},{17,25},{25,17},{2,10},{10... | collective-permute-start | bytes 12582920 | tf_op jit(solution)/shard_map/ppermute | solution.py:300
  323.0 67.3 %collective-permute-start.7 = (bf16[18,8,5120]{2,1,0:T(8,128)(2,1)}, bf16[18,8,5120]{2,1,0:T(8,128)(2,1)}, u32[]{:S(2)}, u32[]{:S(2)}) collective-permute-start(bf16[18,8,5120]{2,1,0:T(8,128)(2,1)} %pick.39), channel_id=1, source_target_pairs={{0,4},{1,5},{2,6},{3,7},{4,0},{5,1},{6,2},{7,3},{8,12},{9,13},{10,... | collective-permute-start | bytes 4423688 | tf_op jit(solution)/shard_map/ppermute | solution.py:181
  395.5 66.4 %all-to-all-start.6 = ((bf16[16,2,8,5120]{3,2,1,0:T(8,128)(2,1)}), bf16[16,2,8,5120]{3,2,1,0:T(8,128)(2,1)S(1)}, u32[]{:S(2)}, u32[]{:S(2)}) async-start(bf16[16,2,8,5120]{3,2,1,0:T(8,128)(2,1)} %bitcast.41), calls=%async_computation.6 | async-start | bytes 5242880 | tf_op jit(solution)/shard_map/all_to_all | solution.py:154
  402.7 50.2 %collective-permute-start.15 = (bf16[1,256,2048]{2,1,0:T(8,128)(2,1)}, bf16[1,256,2048]{2,1,0:T(8,128)(2,1)}, u32[]{:S(2)}, u32[]{:S(2)}) collective-permute-start(bf16[1,256,2048]{2,1,0:T(8,128)(2,1)} %fusion), channel_id=1, source_target_pairs={{0,16},{8,24},{16,0},{24,8},{1,17},{9,25},{17,1},{25,9},{2,18},{10... | collective-permute-start | bytes 3145736 | tf_op jit(solution)/shard_map/ppermute | solution.py:300
  407.5 49.9 %collective-permute-start.6 = (bf16[18,8,3072]{2,1,0:T(8,128)(2,1)}, bf16[18,8,3072]{2,1,0:T(8,128)(2,1)S(1)}, u32[]{:S(2)}, u32[]{:S(2)}) collective-permute-start(bf16[18,8,3072]{2,1,0:T(8,128)(2,1)} %pick.38), channel_id=1, source_target_pairs={{0,4},{1,5},{2,6},{3,7},{4,0},{5,1},{6,2},{7,3},{8,12},{9,13},{10,... | collective-permute-start | bytes 2654216 | tf_op jit(solution)/shard_map/ppermute | solution.py:181
  461.9 72.6 %all-to-all-start.7 = ((bf16[16,2,8,3072]{3,2,1,0:T(8,128)(2,1)}), bf16[16,2,8,3072]{3,2,1,0:T(8,128)(2,1)}, u32[]{:S(2)}, u32[]{:S(2)}) async-start(bf16[16,2,8,3072]{3,2,1,0:T(8,128)(2,1)} %bitcast.44), calls=%async_computation.7 | async-start | bytes 3145728 | tf_op jit(solution)/shard_map/all_to_all | solution.py:154
  469.2 42.4 %copy-start.3 = (f32[1,256,2048]{2,1,0:T(8,128)S(1)}, f32[1,256,2048]{2,1,0:T(8,128)}, u32[]{:S(2)}) copy-start(f32[1,256,2048]{2,1,0:T(8,128)} %fusion.1) | copy-start | bytes 6291460
  470.7 40.9 %collective-permute-start.16 = (f32[128,2048]{1,0:T(8,128)S(1)}, f32[128,2048]{1,0:T(8,128)S(1)}, u32[]{:S(2)}, u32[]{:S(2)}) collective-permute-start(f32[128,2048]{1,0:T(8,128)S(1)} %slice_bitcast_fusion), channel_id=1, source_target_pairs={{0,1},{1,0},{2,3},{3,2},{4,5},{5,4},{6,7},{7,6},{8,9},{9,8},{10,11... | collective-permute-start | bytes 3145736 | tf_op jit(solution)/shard_map/ppermute | solution.py:310
  511.7 7.8 %collective-permute-start.17 = (bf16[64,2048]{1,0:T(8,128)(2,1)S(1)}, bf16[64,2048]{1,0:T(8,128)(2,1)S(1)}, u32[]{:S(2)}, u32[]{:S(2)}) collective-permute-start(bf16[64,2048]{1,0:T(8,128)(2,1)S(1)} %split.48), channel_id=1, source_target_pairs={{0,2},{1,3},{2,0},{3,1},{4,6},{5,7},{6,4},{7,5},{8,10},{9,11},{10,... | collective-permute-start | bytes 786440 | tf_op jit(solution)/shard_map/ppermute | solution.py:310
  519.6 7.9 %collective-permute-start.18 = (bf16[32,2048]{1,0:T(8,128)(2,1)S(1)}, bf16[32,2048]{1,0:T(8,128)(2,1)S(1)}, u32[]{:S(2)}, u32[]{:S(2)}) collective-permute-start(bf16[32,2048]{1,0:T(8,128)(2,1)S(1)} %split.49), channel_id=1, source_target_pairs={{0,4},{1,5},{2,6},{3,7},{4,0},{5,1},{6,2},{7,3},{8,12},{9,13},{10,... | collective-permute-start | bytes 393224 | tf_op jit(solution)/shard_map/ppermute | solution.py:310
  (8 other events, 72.9 us)
